TPU v7x, 32 devices: a whole 2x2x4 slice. The times are simulated.
32 devices in a mesh: gx: 8 (over z, y), gy: 4 (over x, core).
Axes of the slice: x: 2, y: 2, z: 4, core: 2. Of those that a mesh axis runs over, the one named last changes fastest.
Arguments:
- checkpoint: float32 [16, 32, 1024], P(None, 'gy', 'gx'), may hold values from -6 to 6
- trajectory: float32 [16, 32, 1024], P(None, 'gy', 'gx'), may hold values from -6 to 6
- adjoint_forcing: float32 [16, 32, 1024], P(None, 'gy', 'gx'), may hold values from -6 to 6
- east_diffusion: float32 [16, 32, 1024], P(None, 'gy', 'gx'), may hold values from 0.1 to 1
- north_diffusion: float32 [16, 32, 1024], P(None, 'gy', 'gx'), may hold values from 0.3 to 3
- east_wind: float32 [16, 32, 1024], P(None, 'gy', 'gx'), may hold values from -0.6 to 0.6
- north_wind: float32 [16, 32, 1024], P(None, 'gy', 'gx'), may hold values from -6 to 6, as said below
- level_diffusion: float32 [16], replicated, may hold values from 0.1 to 1
- damping: float32 [16], replicated, may hold values from 0.2 to 2
- source: float32 [16, 32, 1024], P(None, 'gy', 'gx'), may hold values from -4 to 5
- observations: float32 [16, 32, 1024], P(None, 'gy', 'gx'), may hold values from -6 to 6
- observation_weight: float32 [16, 32, 1024], P(None, 'gy', 'gx'), may hold values from 0.1 to 1
- step_index: int32 [1], replicated, may hold values from 0 to 95
Outputs:
- forward_state: float32 [16, 32, 1024], P(None, 'gy', 'gx')
- forward_residual: float32 [16, 32, 1024], P(None, 'gy', 'gx')
- adjoint_state: float32 [16, 32, 1024], P(None, 'gy', 'gx')
Inputs may be any that keep to these rules, and one draw needn't show every extreme that they name: At every face the magnitude of north_wind is at most twice north_diffusion.
All inputs are finite; a program needn't handle non-finite values.
Results may differ from a plain program's by a relative error of at most 0.000091.
Values sent between devices are 32-bit elements; how exact they have to be, the bound alone decides.
A program may use at most 64 MiB of HBM per device.

v0:
```python
import math

import jax
import jax.numpy as jnp
from jax import lax
from jax.sharding import PartitionSpec as P

OUTER = 2
INNER = 4
DAY_STEPS = 96


RELAXATION = 0.7


def extended(block, sides, width, periodic):
    for axis, dim in sides:
        count = lax.axis_size(axis)
        forward = [(i, i + 1) for i in range(count - 1)]
        if periodic:
            forward.append((count - 1, 0))
        backward = [(target, source) for source, target in forward]
        low = lax.ppermute(
            lax.slice_in_dim(block, block.shape[dim] - width, None, axis=dim), axis, forward
        )
        high = lax.ppermute(lax.slice_in_dim(block, 0, width, axis=dim), axis, backward)
        block = jnp.concatenate([low, block, high], axis=dim)
    return block


def shifted(array, axis, by):
    size = lax.axis_size(axis)
    return lax.ppermute(array, axis, [(i, (i + by) % size) for i in range(size)])


def shifted_2(block, axis, distance):
    devices = range(lax.axis_size(axis))
    route = [(i - distance, i) for i in devices if i - distance in devices]
    return lax.ppermute(block, axis, route)


def vertical_part(field, up_coef):
    zero_level = jnp.zeros_like(field[:1])
    padded = jnp.concatenate([zero_level, field, zero_level], axis=0)
    flux = up_coef[:, None, None] * (padded[1:] - padded[:-1])
    return -(flux[1:] - flux[:-1])


def apply_forward(west_east, south_north, field, faces):
    east_coef, east_flow, north_coef, north_flow, up_coef = faces
    flux_east = east_flow * (west_east[..., 1:] + west_east[..., :-1]) * 0.5 - east_coef * (
        west_east[..., 1:] - west_east[..., :-1]
    )
    flux_north = north_flow * (south_north[:, 1:] + south_north[:, :-1]) * 0.5 - north_coef * (
        south_north[:, 1:] - south_north[:, :-1]
    )
    return (
        flux_east[..., 1:]
        - flux_east[..., :-1]
        + (flux_north[:, 1:] - flux_north[:, :-1])
        + vertical_part(field, up_coef)
    )


def scatter_parts(field, faces):
    east_coef, east_flow, north_coef, north_flow, up_coef = faces
    padded_east = jnp.pad(field, ((0, 0), (0, 0), (1, 1)))
    weight_east = padded_east[..., :-1] - padded_east[..., 1:]
    spread_east = jnp.pad(weight_east * (east_flow * 0.5 + east_coef), ((0, 0), (0, 0), (0, 1)))
    spread_east = spread_east + jnp.pad(
        weight_east * (east_flow * 0.5 - east_coef), ((0, 0), (0, 0), (1, 0))
    )
    padded_north = jnp.pad(field, ((0, 0), (1, 1), (0, 0)))
    weight_north = padded_north[:, :-1] - padded_north[:, 1:]
    spread_north = jnp.pad(weight_north * (north_flow * 0.5 + north_coef), ((0, 0), (0, 1), (0, 0)))
    spread_north = spread_north + jnp.pad(
        weight_north * (north_flow * 0.5 - north_coef), ((0, 0), (1, 0), (0, 0))
    )
    middle = spread_east[..., 1:-1] + spread_north[:, 1:-1] + vertical_part(field, up_coef)
    blank_east = jnp.zeros_like(field[..., 2:])
    rim_east = jnp.concatenate([spread_east[..., :1], blank_east, spread_east[..., -1:]], axis=2)
    blank_north = jnp.zeros_like(field[:, 2:])
    rim_north = jnp.concatenate([spread_north[:, :1], blank_north, spread_north[:, -1:]], axis=1)
    return (middle, rim_east, rim_north)


def scatter_finish(middle, west_east, south_north):
    blank_east = jnp.zeros_like(middle[..., 2:])
    arrived_east = jnp.concatenate([west_east[..., :1], blank_east, west_east[..., -1:]], axis=2)
    blank_north = jnp.zeros_like(middle[:, 2:])
    arrived_north = jnp.concatenate([south_north[:, :1], blank_north, south_north[:, -1:]], axis=1)
    return middle + arrived_east + arrived_north


def diagonal_of(tangent, faces, damping):
    east_coef, east_flow, north_coef, north_flow, up_coef = faces
    total = 1.0 + east_coef[..., 1:] + east_coef[..., :-1] + north_coef[:, 1:] + north_coef[:, :-1]
    total = total + (up_coef[1:] + up_coef[:-1])[:, None, None]
    return total + damping[:, None, None] * (1.0 - tangent * tangent)


def lon_extend(stacked):
    return extended(stacked, (("gx", 3),), 1, True)


def lat_extend(stacked):
    return extended(stacked, (("gy", 2),), 1, False)


def run_tasks(tasks):
    west_east = lon_extend(jnp.stack([pending[0] for pending in tasks]))
    south_north = lat_extend(jnp.stack([pending[1] for pending in tasks]))
    return [
        pending[2](west_east[number], south_north[number]) for number, pending in enumerate(tasks)
    ]


def per_device(
    checkpoint,
    trajectory,
    adjoint_forcing,
    east_diffusion,
    north_diffusion,
    east_wind,
    north_wind,
    level_diffusion,
    damping,
    source,
    observations,
    observation_weight,
    step_index,
):
    levels, lat_rows, lon_cols = checkpoint.shape
    row_global = lax.axis_index("gy") * lat_rows + jnp.arange(lat_rows, dtype=jnp.int32)
    row_mask = (row_global < lat_rows * lax.axis_size("gy") - 1).astype(jnp.float32)[None, :, None]
    level_mask = (jnp.arange(levels) < levels - 1).astype(jnp.float32)
    north_masked = north_diffusion * row_mask
    flow_masked = north_wind * row_mask
    up_coef = jnp.concatenate([jnp.zeros_like(level_diffusion[:1]), level_diffusion * level_mask])
    column = (lax.axis_index("gx") * lon_cols + jnp.arange(lon_cols, dtype=jnp.int32)).astype(
        jnp.float32
    )
    phase = (
        2.0 * math.pi * column / (lon_cols * lax.axis_size("gx"))
        - 2.0 * math.pi * step_index[0].astype(jnp.float32) / DAY_STEPS
    )
    forcing = source * jnp.cos(phase)[None, None, :]
    damp = damping[:, None, None]
    edge_west = shifted(jnp.stack([east_diffusion[..., -1:], east_wind[..., -1:]]), "gx", 1)
    edge_south = shifted_2(jnp.stack([north_masked[:, -1:], flow_masked[:, -1:]]), "gy", 1)
    faces = (
        jnp.concatenate([edge_west[0], east_diffusion], axis=2),
        jnp.concatenate([edge_west[1], east_wind], axis=2),
        jnp.concatenate([edge_south[0], north_masked], axis=1),
        jnp.concatenate([edge_south[1], flow_masked], axis=1),
        up_coef,
    )

    def forward_task(field):
        return (
            field,
            field,
            lambda west_east, south_north: apply_forward(west_east, south_north, field, faces),
        )

    def adjoint_task(field):
        middle, rim_east, rim_north = scatter_parts(field, faces)
        return (
            rim_east,
            rim_north,
            lambda west_east, south_north: scatter_finish(middle, west_east, south_north),
        )

    forward = {"state": checkpoint}

    def forward_update(section, closing, applied):
        if section == "res":
            state = forward["state"]
            tangent = jnp.tanh(state)
            diagonal = diagonal_of(tangent, faces, damping)
            resid = state - checkpoint + applied + damp * tangent - forcing
            forward["tangent"] = tangent
            forward["diagonal"] = diagonal
            forward["resid"] = resid
            forward["delta"] = -RELAXATION * resid / diagonal
        elif section == "lin":
            tangent = forward["tangent"]
            delta = forward["delta"]
            image = delta + applied + damp * (1.0 - tangent * tangent) * delta
            forward["delta"] = (
                delta + RELAXATION * (-forward["resid"] - image) / forward["diagonal"]
            )
        else:
            state = forward["state"]
            forward["final"] = state - checkpoint + applied + damp * jnp.tanh(state) - forcing
        if closing:
            forward["state"] = forward["state"] + forward["delta"]

    tangent_n = jnp.tanh(trajectory)
    diagonal_n = diagonal_of(tangent_n, faces, damping)
    local_n = damp * (1.0 - tangent_n * tangent_n)
    start_resid = -adjoint_forcing
    adjoint = {
        "mult": jnp.zeros_like(trajectory),
        "resid": start_resid,
        "delta": -RELAXATION * start_resid / diagonal_n,
    }

    def adjoint_update(section, closing, applied):
        if section == "res":
            multiplier = adjoint["mult"]
            resid = multiplier + applied + local_n * multiplier - adjoint_forcing
            adjoint["resid"] = resid
            adjoint["delta"] = -RELAXATION * resid / diagonal_n
        else:
            delta = adjoint["delta"]
            image = delta + applied + local_n * delta
            adjoint["delta"] = delta + RELAXATION * (-adjoint["resid"] - image) / diagonal_n
        if closing:
            adjoint["mult"] = adjoint["mult"] + adjoint["delta"]

    forward_plan = []
    adjoint_plan = []
    for newton_step in range(OUTER):
        forward_plan.append(("res", INNER == 1))
        if newton_step > 0:
            adjoint_plan.append(("res", INNER == 1))
        for inner_step in range(INNER - 1):
            forward_plan.append(("lin", inner_step == INNER - 2))
            adjoint_plan.append(("lin", inner_step == INNER - 2))
    forward_plan.append(("final", False))
    for position in range(max(len(forward_plan), len(adjoint_plan))):
        pending_tasks = []
        pending_tasks.append(
            forward_task(
                forward["delta"] if forward_plan[position][0] == "lin" else forward["state"]
            )
        )
        if position < len(adjoint_plan):
            pending_tasks.append(
                adjoint_task(
                    adjoint["delta"] if adjoint_plan[position][0] == "lin" else adjoint["mult"]
                )
            )
        results = run_tasks(pending_tasks)
        offset = 0
        forward_update(forward_plan[position][0], forward_plan[position][1], results[0])
        offset = 1
        if position < len(adjoint_plan):
            adjoint_update(adjoint_plan[position][0], adjoint_plan[position][1], results[offset])
    final_state = forward["state"]
    final_resid = forward["final"]
    multiplier = adjoint["mult"]
    adjoint_state = multiplier + observation_weight * (final_state - observations)
    return (final_state, final_resid, adjoint_state)


def solution(mesh):
    in_specs = (
        P(None, "gy", "gx"),
        P(None, "gy", "gx"),
        P(None, "gy", "gx"),
        P(None, "gy", "gx"),
        P(None, "gy", "gx"),
        P(None, "gy", "gx"),
        P(None, "gy", "gx"),
        P(),
        P(),
        P(None, "gy", "gx"),
        P(None, "gy", "gx"),
        P(None, "gy", "gx"),
        P(),
    )
    out_specs = (P(None, "gy", "gx"), P(None, "gy", "gx"), P(None, "gy", "gx"))
    return jax.shard_map(
        per_device, mesh=mesh, in_specs=in_specs, out_specs=out_specs, check_vma=False
    )
```

profile of v0, /device:TPU:1, one launch (start us, length us, event | category | flops | bytes accessed | tf_op | source)
XLA Modules:
  0.0 133.0 jit_solution(8044564972937422314)
XLA Ops:
  1.7 4.5 %collective-permute-start.1 = (f32[2,16,1,128]{3,1,2,0:T(8,128)S(1)}, f32[2,16,1,128]{3,1,2,0:T(8,128)S(1)}, u32[]{:S(2)}, u32[]{:S(2)}) collective-permute-start(f32[2,16,1,128]{3,1,2,0:T(8,128)S(1)} %pad_maximum_fusion.32), channel_id=1, source_target_pairs={{0,1},{1,2},{2,3},{4,5},{5,6},{6,7},{8,9},{9,10},{10,11},{12,13},{... | collective-permute-start | bytes 49160 | tf_op jit(solution)/shard_map/ppermute | solution.py:39
  9.7 3.1 %collective-permute-done = f32[2,16,8,1]{1,2,3,0:T(8,128)S(1)} collective-permute-done((f32[2,16,8,1]{1,2,3,0:T(8,128)S(1)}, f32[2,16,8,1]{1,2,3,0:T(8,128)S(1)}, u32[]{:S(2)}, u32[]{:S(2)}) %collective-permute-start) | collective-permute-done | bytes 1056 | tf_op jit(solution)/shard_map/ppermute | solution.py:33
  15.2 4.1 %collective-permute-start.3 = (f32[2,16,8,1]{3,2,1,0:T(8,128)S(1)}, f32[2,16,8,1]{3,2,1,0:T(8,128)S(1)}, u32[]{:S(2)}, u32[]{:S(2)}) collective-permute-start(f32[2,16,8,1]{3,2,1,0:T(8,128)S(1)} %get-tuple-element.150), channel_id=1, source_target_pairs={{4,0},{8,4},{12,8},{16,12},{20,16},{24,20},{28,24},{0,28},{5,1},{9... | collective-permute-start | bytes 3080 | tf_op jit(solution)/shard_map/ppermute | solution.py:26
  19.5 3.5 %collective-permute-start.4 = (f32[2,16,1,128]{3,2,1,0:T(1,128)S(1)}, f32[2,16,1,128]{3,2,1,0:T(1,128)S(1)}, u32[]{:S(2)}, u32[]{:S(2)}) collective-permute-start(f32[2,16,1,128]{3,2,1,0:T(1,128)S(1)} %get-tuple-element.145), channel_id=1, source_target_pairs={{0,1},{1,2},{2,3},{4,5},{5,6},{6,7},{8,9},{9,10},{10,11},{12,13},{... | collective-permute-start | bytes 49160 | tf_op jit(solution)/shard_map/ppermute | solution.py:23
  25.5 2.6 %collective-permute-done.5 = f32[2,16,1,128]{3,2,1,0:T(1,128)S(1)} collective-permute-done((f32[2,16,1,128]{3,2,1,0:T(1,128)S(1)}, f32[2,16,1,128]{3,2,1,0:T(1,128)S(1)}, u32[]{:S(2)}, u32[]{:S(2)}) %collective-permute-start.5) | collective-permute-done | bytes 16416 | tf_op jit(solution)/shard_map/ppermute | solution.py:26
  29.9 4.1 %collective-permute-start.7 = (f32[2,16,8,1]{3,2,1,0:T(8,128)S(1)}, f32[2,16,8,1]{3,2,1,0:T(8,128)S(1)}, u32[]{:S(2)}, u32[]{:S(2)}) collective-permute-start(f32[2,16,8,1]{3,2,1,0:T(8,128)S(1)} %get-tuple-element.142), channel_id=1, source_target_pairs={{4,0},{8,4},{12,8},{16,12},{20,16},{24,20},{28,24},{0,28},{5,1},{9... | collective-permute-start | bytes 3080 | tf_op jit(solution)/shard_map/ppermute | solution.py:26
  34.2 2.5 %collective-permute-start.8 = (f32[2,16,1,128]{3,2,1,0:T(1,128)S(1)}, f32[2,16,1,128]{3,2,1,0:T(1,128)S(1)}, u32[]{:S(2)}, u32[]{:S(2)}) collective-permute-start(f32[2,16,1,128]{3,2,1,0:T(1,128)S(1)} %get-tuple-element.137), channel_id=1, source_target_pairs={{0,1},{1,2},{2,3},{4,5},{5,6},{6,7},{8,9},{9,10},{10,11},{12,13},{... | collective-permute-start | bytes 49160 | tf_op jit(solution)/shard_map/ppermute | solution.py:23
  39.1 2.6 %collective-permute-done.9 = f32[2,16,1,128]{3,2,1,0:T(1,128)S(1)} collective-permute-done((f32[2,16,1,128]{3,2,1,0:T(1,128)S(1)}, f32[2,16,1,128]{3,2,1,0:T(1,128)S(1)}, u32[]{:S(2)}, u32[]{:S(2)}) %collective-permute-start.9) | collective-permute-done | bytes 16416 | tf_op jit(solution)/shard_map/ppermute | solution.py:26
  42.8 4.1 %collective-permute-start.11 = (f32[2,16,8,1]{3,2,1,0:T(8,128)S(1)}, f32[2,16,8,1]{3,2,1,0:T(8,128)S(1)}, u32[]{:S(2)}, u32[]{:S(2)}) collective-permute-start(f32[2,16,8,1]{3,2,1,0:T(8,128)S(1)} %get-tuple-element.134), channel_id=1, source_target_pairs={{4,0},{8,4},{12,8},{16,12},{20,16},{24,20},{28,24},{0,28},{5,1},{9... | collective-permute-start | bytes 3080 | tf_op jit(solution)/shard_map/ppermute | solution.py:26
  47.1 2.5 %collective-permute-start.12 = (f32[2,16,1,128]{3,2,1,0:T(1,128)S(1)}, f32[2,16,1,128]{3,2,1,0:T(1,128)S(1)}, u32[]{:S(2)}, u32[]{:S(2)}) collective-permute-start(f32[2,16,1,128]{3,2,1,0:T(1,128)S(1)} %get-tuple-element.129), channel_id=1, source_target_pairs={{0,1},{1,2},{2,3},{4,5},{5,6},{6,7},{8,9},{9,10},{10,11},{12,13},{... | collective-permute-start | bytes 49160 | tf_op jit(solution)/shard_map/ppermute | solution.py:23
  49.6 1.9 %collective-permute-start.13 = (f32[2,16,1,128]{3,2,1,0:T(1,128)S(1)}, f32[2,16,1,128]{3,2,1,0:T(1,128)S(1)}, u32[]{:S(2)}, u32[]{:S(2)}) collective-permute-start(f32[2,16,1,128]{3,2,1,0:T(1,128)S(1)} %get-tuple-element.130), channel_id=1, source_target_pairs={{1,0},{2,1},{3,2},{5,4},{6,5},{7,6},{9,8},{10,9},{11,10},{13,12},{... | collective-permute-start | bytes 49160 | tf_op jit(solution)/shard_map/ppermute | solution.py:26
  52.0 2.6 %collective-permute-done.13 = f32[2,16,1,128]{3,2,1,0:T(1,128)S(1)} collective-permute-done((f32[2,16,1,128]{3,2,1,0:T(1,128)S(1)}, f32[2,16,1,128]{3,2,1,0:T(1,128)S(1)}, u32[]{:S(2)}, u32[]{:S(2)}) %collective-permute-start.13) | collective-permute-done | bytes 16416 | tf_op jit(solution)/shard_map/ppermute | solution.py:26
  55.7 4.1 %collective-permute-start.15 = (f32[2,16,8,1]{3,2,1,0:T(8,128)S(1)}, f32[2,16,8,1]{3,2,1,0:T(8,128)S(1)}, u32[]{:S(2)}, u32[]{:S(2)}) collective-permute-start(f32[2,16,8,1]{3,2,1,0:T(8,128)S(1)} %get-tuple-element.122), channel_id=1, source_target_pairs={{4,0},{8,4},{12,8},{16,12},{20,16},{24,20},{28,24},{0,28},{5,1},{9... | collective-permute-start | bytes 3080 | tf_op jit(solution)/shard_map/ppermute | solution.py:26
  60.0 2.5 %collective-permute-start.16 = (f32[2,16,1,128]{3,2,1,0:T(1,128)S(1)}, f32[2,16,1,128]{3,2,1,0:T(1,128)S(1)}, u32[]{:S(2)}, u32[]{:S(2)}) collective-permute-start(f32[2,16,1,128]{3,2,1,0:T(1,128)S(1)} %get-tuple-element.125), channel_id=1, source_target_pairs={{0,1},{1,2},{2,3},{4,5},{5,6},{6,7},{8,9},{9,10},{10,11},{12,13},{... | collective-permute-start | bytes 49160 | tf_op jit(solution)/shard_map/ppermute | solution.py:23
  62.5 1.9 %collective-permute-start.17 = (f32[2,16,1,128]{3,2,1,0:T(1,128)S(1)}, f32[2,16,1,128]{3,2,1,0:T(1,128)S(1)}, u32[]{:S(2)}, u32[]{:S(2)}) collective-permute-start(f32[2,16,1,128]{3,2,1,0:T(1,128)S(1)} %get-tuple-element.126), channel_id=1, source_target_pairs={{1,0},{2,1},{3,2},{5,4},{6,5},{7,6},{9,8},{10,9},{11,10},{13,12},{... | collective-permute-start | bytes 49160 | tf_op jit(solution)/shard_map/ppermute | solution.py:26
  64.9 2.6 %collective-permute-done.17 = f32[2,16,1,128]{3,2,1,0:T(1,128)S(1)} collective-permute-done((f32[2,16,1,128]{3,2,1,0:T(1,128)S(1)}, f32[2,16,1,128]{3,2,1,0:T(1,128)S(1)}, u32[]{:S(2)}, u32[]{:S(2)}) %collective-permute-start.17) | collective-permute-done | bytes 16416 | tf_op jit(solution)/shard_map/ppermute | solution.py:26
  68.7 4.1 %collective-permute-start.19 = (f32[2,16,8,1]{3,2,1,0:T(8,128)S(1)}, f32[2,16,8,1]{3,2,1,0:T(8,128)S(1)}, u32[]{:S(2)}, u32[]{:S(2)}) collective-permute-start(f32[2,16,8,1]{3,2,1,0:T(8,128)S(1)} %get-tuple-element.118), channel_id=1, source_target_pairs={{4,0},{8,4},{12,8},{16,12},{20,16},{24,20},{28,24},{0,28},{5,1},{9... | collective-permute-start | bytes 3080 | tf_op jit(solution)/shard_map/ppermute | solution.py:26
  72.9 2.5 %collective-permute-start.20 = (f32[2,16,1,128]{3,2,1,0:T(1,128)S(1)}, f32[2,16,1,128]{3,2,1,0:T(1,128)S(1)}, u32[]{:S(2)}, u32[]{:S(2)}) collective-permute-start(f32[2,16,1,128]{3,2,1,0:T(1,128)S(1)} %get-tuple-element.113), channel_id=1, source_target_pairs={{0,1},{1,2},{2,3},{4,5},{5,6},{6,7},{8,9},{9,10},{10,11},{12,13},{... | collective-permute-start | bytes 49160 | tf_op jit(solution)/shard_map/ppermute | solution.py:23
  77.9 2.6 %collective-permute-done.21 = f32[2,16,1,128]{3,2,1,0:T(1,128)S(1)} collective-permute-done((f32[2,16,1,128]{3,2,1,0:T(1,128)S(1)}, f32[2,16,1,128]{3,2,1,0:T(1,128)S(1)}, u32[]{:S(2)}, u32[]{:S(2)}) %collective-permute-start.21) | collective-permute-done | bytes 16416 | tf_op jit(solution)/shard_map/ppermute | solution.py:26
  81.6 4.1 %collective-permute-start.23 = (f32[2,16,8,1]{3,2,1,0:T(8,128)S(1)}, f32[2,16,8,1]{3,2,1,0:T(8,128)S(1)}, u32[]{:S(2)}, u32[]{:S(2)}) collective-permute-start(f32[2,16,8,1]{3,2,1,0:T(8,128)S(1)} %get-tuple-element.110), channel_id=1, source_target_pairs={{4,0},{8,4},{12,8},{16,12},{20,16},{24,20},{28,24},{0,28},{5,1},{9... | collective-permute-start | bytes 3080 | tf_op jit(solution)/shard_map/ppermute | solution.py:26
  85.9 2.5 %collective-permute-start.24 = (f32[2,16,1,128]{3,2,1,0:T(1,128)S(1)}, f32[2,16,1,128]{3,2,1,0:T(1,128)S(1)}, u32[]{:S(2)}, u32[]{:S(2)}) collective-permute-start(f32[2,16,1,128]{3,2,1,0:T(1,128)S(1)} %get-tuple-element.105), channel_id=1, source_target_pairs={{0,1},{1,2},{2,3},{4,5},{5,6},{6,7},{8,9},{9,10},{10,11},{12,13},{... | collective-permute-start | bytes 49160 | tf_op jit(solution)/shard_map/ppermute | solution.py:23
  90.8 2.6 %collective-permute-done.25 = f32[2,16,1,128]{3,2,1,0:T(1,128)S(1)} collective-permute-done((f32[2,16,1,128]{3,2,1,0:T(1,128)S(1)}, f32[2,16,1,128]{3,2,1,0:T(1,128)S(1)}, u32[]{:S(2)}, u32[]{:S(2)}) %collective-permute-start.25) | collective-permute-done | bytes 16416 | tf_op jit(solution)/shard_map/ppermute | solution.py:26
  94.5 4.1 %collective-permute-start.27 = (f32[2,16,8,1]{3,2,1,0:T(8,128)S(1)}, f32[2,16,8,1]{3,2,1,0:T(8,128)S(1)}, u32[]{:S(2)}, u32[]{:S(2)}) collective-permute-start(f32[2,16,8,1]{3,2,1,0:T(8,128)S(1)} %get-tuple-element.102), channel_id=1, source_target_pairs={{4,0},{8,4},{12,8},{16,12},{20,16},{24,20},{28,24},{0,28},{5,1},{9... | collective-permute-start | bytes 3080 | tf_op jit(solution)/shard_map/ppermute | solution.py:26
  98.8 2.5 %collective-permute-start.28 = (f32[2,16,1,128]{3,2,1,0:T(1,128)S(1)}, f32[2,16,1,128]{3,2,1,0:T(1,128)S(1)}, u32[]{:S(2)}, u32[]{:S(2)}) collective-permute-start(f32[2,16,1,128]{3,2,1,0:T(1,128)S(1)} %get-tuple-element.97), channel_id=1, source_target_pairs={{0,1},{1,2},{2,3},{4,5},{5,6},{6,7},{8,9},{9,10},{10,11},{12,13},{... | collective-permute-start | bytes 49160 | tf_op jit(solution)/shard_map/ppermute | solution.py:23
  101.3 1.9 %collective-permute-start.29 = (f32[2,16,1,128]{3,2,1,0:T(1,128)S(1)}, f32[2,16,1,128]{3,2,1,0:T(1,128)S(1)}, u32[]{:S(2)}, u32[]{:S(2)}) collective-permute-start(f32[2,16,1,128]{3,2,1,0:T(1,128)S(1)} %get-tuple-element.98), channel_id=1, source_target_pairs={{1,0},{2,1},{3,2},{5,4},{6,5},{7,6},{9,8},{10,9},{11,10},{13,12},{... | collective-permute-start | bytes 49160 | tf_op jit(solution)/shard_map/ppermute | solution.py:26
  103.7 2.6 %collective-permute-done.29 = f32[2,16,1,128]{3,2,1,0:T(1,128)S(1)} collective-permute-done((f32[2,16,1,128]{3,2,1,0:T(1,128)S(1)}, f32[2,16,1,128]{3,2,1,0:T(1,128)S(1)}, u32[]{:S(2)}, u32[]{:S(2)}) %collective-permute-start.29) | collective-permute-done | bytes 16416 | tf_op jit(solution)/shard_map/ppermute | solution.py:26
  106.9 4.1 %collective-permute-start.31 = (f32[1,16,8,1]{3,2,1,0:T(8,128)S(1)}, f32[1,16,8,1]{3,2,1,0:T(8,128)S(1)}, u32[]{:S(2)}, u32[]{:S(2)}) collective-permute-start(f32[1,16,8,1]{3,2,1,0:T(8,128)S(1)} %get-tuple-element.156), channel_id=1, source_target_pairs={{4,0},{8,4},{12,8},{16,12},{20,16},{24,20},{28,24},{0,28},{5,1},{9... | collective-permute-start | bytes 1544 | tf_op jit(solution)/shard_map/ppermute | solution.py:26
  111.0 2.5 %collective-permute-start.32 = (f32[1,16,1,128]{3,2,1,0:T(1,128)S(1)}, f32[1,16,1,128]{3,2,1,0:T(1,128)S(1)}, u32[]{:S(2)}, u32[]{:S(2)}) collective-permute-start(f32[1,16,1,128]{3,2,1,0:T(1,128)S(1)} %get-tuple-element.157), channel_id=1, source_target_pairs={{0,1},{1,2},{2,3},{4,5},{5,6},{6,7},{8,9},{9,10},{10,11},{12,13},{... | collective-permute-start | bytes 24584 | tf_op jit(solution)/shard_map/ppermute | solution.py:23
  115.8 2.7 %collective-permute-done.33 = f32[1,16,1,128]{3,2,1,0:T(1,128)S(1)} collective-permute-done((f32[1,16,1,128]{3,2,1,0:T(1,128)S(1)}, f32[1,16,1,128]{3,2,1,0:T(1,128)S(1)}, u32[]{:S(2)}, u32[]{:S(2)}) %collective-permute-start.33) | collective-permute-done | bytes 8224 | tf_op jit(solution)/shard_map/ppermute | solution.py:26
  120.4 4.1 %collective-permute-start.35 = (f32[1,16,8,1]{3,2,1,0:T(8,128)S(1)}, f32[1,16,8,1]{3,2,1,0:T(8,128)S(1)}, u32[]{:S(2)}, u32[]{:S(2)}) collective-permute-start(f32[1,16,8,1]{3,2,1,0:T(8,128)S(1)} %get-tuple-element.152), channel_id=1, source_target_pairs={{4,0},{8,4},{12,8},{16,12},{20,16},{24,20},{28,24},{0,28},{5,1},{9... | collective-permute-start | bytes 1544 | tf_op jit(solution)/shard_map/ppermute | solution.py:26
  124.6 2.5 %collective-permute-start.36 = (f32[1,16,1,128]{3,2,1,0:T(1,128)S(1)}, f32[1,16,1,128]{3,2,1,0:T(1,128)S(1)}, u32[]{:S(2)}, u32[]{:S(2)}) collective-permute-start(f32[1,16,1,128]{3,2,1,0:T(1,128)S(1)} %get-tuple-element.153), channel_id=1, source_target_pairs={{0,1},{1,2},{2,3},{4,5},{5,6},{6,7},{8,9},{9,10},{10,11},{12,13},{... | collective-permute-start | bytes 24584 | tf_op jit(solution)/shard_map/ppermute | solution.py:23
  129.4 2.7 %collective-permute-done.37 = f32[1,16,1,128]{3,2,1,0:T(1,128)S(1)} collective-permute-done((f32[1,16,1,128]{3,2,1,0:T(1,128)S(1)}, f32[1,16,1,128]{3,2,1,0:T(1,128)S(1)}, u32[]{:S(2)}, u32[]{:S(2)}) %collective-permute-start.37) | collective-permute-done | bytes 8224 | tf_op jit(solution)/shard_map/ppermute | solution.py:26
  (235 shorter events, 32.3 us)
Async XLA Ops:
  1.7 11.3 %collective-permute-start.1 = (f32[2,16,1,128]{3,1,2,0:T(8,128)S(1)}, f32[2,16,1,128]{3,1,2,0:T(8,128)S(1)}, u32[]{:S(2)}, u32[]{:S(2)}) collective-permute-start(f32[2,16,1,128]{3,1,2,0:T(8,128)S(1)} %pad_maximum_fusion.32), channel_id=1, source_target_pairs={{0,1},{1,2},{2,3},{4,5},{5,6},{6,7},{8,9},{9,10},{10,11},{12,13},{... | collective-permute-start | bytes 49160 | tf_op jit(solution)/shard_map/ppermute | solution.py:39
  7.4 5.4 %collective-permute-start = (f32[2,16,8,1]{1,2,3,0:T(8,128)S(1)}, f32[2,16,8,1]{1,2,3,0:T(8,128)S(1)}, u32[]{:S(2)}, u32[]{:S(2)}) collective-permute-start(f32[2,16,8,1]{1,2,3,0:T(8,128)S(1)} %pad_maximum_fusion.33), channel_id=1, source_target_pairs={{0,4},{4,8},{8,12},{12,16},{16,20},{20,24},{24,28},{28,0},{1,5},{5... | collective-permute-start | bytes 3080 | tf_op jit(solution)/shard_map/ppermute | solution.py:33
  15.1 9.9 %collective-permute-start.2 = (f32[2,16,8,1]{3,2,1,0:T(8,128)S(1)}, f32[2,16,8,1]{3,2,1,0:T(8,128)S(1)}, u32[]{:S(2)}, u32[]{:S(2)}) collective-permute-start(f32[2,16,8,1]{3,2,1,0:T(8,128)S(1)} %get-tuple-element.149), channel_id=1, source_target_pairs={{0,4},{4,8},{8,12},{12,16},{16,20},{20,24},{24,28},{28,0},{1,5},{5... | collective-permute-start | bytes 3080 | tf_op jit(solution)/shard_map/ppermute | solution.py:23
  15.2 9.8 %collective-permute-start.3 = (f32[2,16,8,1]{3,2,1,0:T(8,128)S(1)}, f32[2,16,8,1]{3,2,1,0:T(8,128)S(1)}, u32[]{:S(2)}, u32[]{:S(2)}) collective-permute-start(f32[2,16,8,1]{3,2,1,0:T(8,128)S(1)} %get-tuple-element.150), channel_id=1, source_target_pairs={{4,0},{8,4},{12,8},{16,12},{20,16},{24,20},{28,24},{0,28},{5,1},{9... | collective-permute-start | bytes 3080 | tf_op jit(solution)/shard_map/ppermute | solution.py:26
  19.5 5.9 %collective-permute-start.4 = (f32[2,16,1,128]{3,2,1,0:T(1,128)S(1)}, f32[2,16,1,128]{3,2,1,0:T(1,128)S(1)}, u32[]{:S(2)}, u32[]{:S(2)}) collective-permute-start(f32[2,16,1,128]{3,2,1,0:T(1,128)S(1)} %get-tuple-element.145), channel_id=1, source_target_pairs={{0,1},{1,2},{2,3},{4,5},{5,6},{6,7},{8,9},{9,10},{10,11},{12,13},{... | collective-permute-start | bytes 49160 | tf_op jit(solution)/shard_map/ppermute | solution.py:23
  23.0 5.1 %collective-permute-start.5 = (f32[2,16,1,128]{3,2,1,0:T(1,128)S(1)}, f32[2,16,1,128]{3,2,1,0:T(1,128)S(1)}, u32[]{:S(2)}, u32[]{:S(2)}) collective-permute-start(f32[2,16,1,128]{3,2,1,0:T(1,128)S(1)} %get-tuple-element.146), channel_id=1, source_target_pairs={{1,0},{2,1},{3,2},{5,4},{6,5},{7,6},{9,8},{10,9},{11,10},{13,12},{... | collective-permute-start | bytes 49160 | tf_op jit(solution)/shard_map/ppermute | solution.py:26
  29.8 8.8 %collective-permute-start.6 = (f32[2,16,8,1]{3,2,1,0:T(8,128)S(1)}, f32[2,16,8,1]{3,2,1,0:T(8,128)S(1)}, u32[]{:S(2)}, u32[]{:S(2)}) collective-permute-start(f32[2,16,8,1]{3,2,1,0:T(8,128)S(1)} %get-tuple-element.141), channel_id=1, source_target_pairs={{0,4},{4,8},{8,12},{12,16},{16,20},{20,24},{24,28},{28,0},{1,5},{5... | collective-permute-start | bytes 3080 | tf_op jit(solution)/shard_map/ppermute | solution.py:23
  29.9 8.7 %collective-permute-start.7 = (f32[2,16,8,1]{3,2,1,0:T(8,128)S(1)}, f32[2,16,8,1]{3,2,1,0:T(8,128)S(1)}, u32[]{:S(2)}, u32[]{:S(2)}) collective-permute-start(f32[2,16,8,1]{3,2,1,0:T(8,128)S(1)} %get-tuple-element.142), channel_id=1, source_target_pairs={{4,0},{8,4},{12,8},{16,12},{20,16},{24,20},{28,24},{0,28},{5,1},{9... | collective-permute-start | bytes 3080 | tf_op jit(solution)/shard_map/ppermute | solution.py:26
  36.7 5.1 %collective-permute-start.9 = (f32[2,16,1,128]{3,2,1,0:T(1,128)S(1)}, f32[2,16,1,128]{3,2,1,0:T(1,128)S(1)}, u32[]{:S(2)}, u32[]{:S(2)}) collective-permute-start(f32[2,16,1,128]{3,2,1,0:T(1,128)S(1)} %get-tuple-element.138), channel_id=1, source_target_pairs={{1,0},{2,1},{3,2},{5,4},{6,5},{7,6},{9,8},{10,9},{11,10},{13,12},{... | collective-permute-start | bytes 49160 | tf_op jit(solution)/shard_map/ppermute | solution.py:26
  42.8 8.8 %collective-permute-start.10 = (f32[2,16,8,1]{3,2,1,0:T(8,128)S(1)}, f32[2,16,8,1]{3,2,1,0:T(8,128)S(1)}, u32[]{:S(2)}, u32[]{:S(2)}) collective-permute-start(f32[2,16,8,1]{3,2,1,0:T(8,128)S(1)} %get-tuple-element.133), channel_id=1, source_target_pairs={{0,4},{4,8},{8,12},{12,16},{16,20},{20,24},{24,28},{28,0},{1,5},{5... | collective-permute-start | bytes 3080 | tf_op jit(solution)/shard_map/ppermute | solution.py:23
  42.8 8.7 %collective-permute-start.11 = (f32[2,16,8,1]{3,2,1,0:T(8,128)S(1)}, f32[2,16,8,1]{3,2,1,0:T(8,128)S(1)}, u32[]{:S(2)}, u32[]{:S(2)}) collective-permute-start(f32[2,16,8,1]{3,2,1,0:T(8,128)S(1)} %get-tuple-element.134), channel_id=1, source_target_pairs={{4,0},{8,4},{12,8},{16,12},{20,16},{24,20},{28,24},{0,28},{5,1},{9... | collective-permute-start | bytes 3080 | tf_op jit(solution)/shard_map/ppermute | solution.py:26
  49.6 5.1 %collective-permute-start.13 = (f32[2,16,1,128]{3,2,1,0:T(1,128)S(1)}, f32[2,16,1,128]{3,2,1,0:T(1,128)S(1)}, u32[]{:S(2)}, u32[]{:S(2)}) collective-permute-start(f32[2,16,1,128]{3,2,1,0:T(1,128)S(1)} %get-tuple-element.130), channel_id=1, source_target_pairs={{1,0},{2,1},{3,2},{5,4},{6,5},{7,6},{9,8},{10,9},{11,10},{13,12},{... | collective-permute-start | bytes 49160 | tf_op jit(solution)/shard_map/ppermute | solution.py:26
  55.7 8.8 %collective-permute-start.14 = (f32[2,16,8,1]{3,2,1,0:T(8,128)S(1)}, f32[2,16,8,1]{3,2,1,0:T(8,128)S(1)}, u32[]{:S(2)}, u32[]{:S(2)}) collective-permute-start(f32[2,16,8,1]{3,2,1,0:T(8,128)S(1)} %get-tuple-element.121), channel_id=1, source_target_pairs={{0,4},{4,8},{8,12},{12,16},{16,20},{20,24},{24,28},{28,0},{1,5},{5... | collective-permute-start | bytes 3080 | tf_op jit(solution)/shard_map/ppermute | solution.py:23
  55.7 8.7 %collective-permute-start.15 = (f32[2,16,8,1]{3,2,1,0:T(8,128)S(1)}, f32[2,16,8,1]{3,2,1,0:T(8,128)S(1)}, u32[]{:S(2)}, u32[]{:S(2)}) collective-permute-start(f32[2,16,8,1]{3,2,1,0:T(8,128)S(1)} %get-tuple-element.122), channel_id=1, source_target_pairs={{4,0},{8,4},{12,8},{16,12},{20,16},{24,20},{28,24},{0,28},{5,1},{9... | collective-permute-start | bytes 3080 | tf_op jit(solution)/shard_map/ppermute | solution.py:26
  62.5 5.1 %collective-permute-start.17 = (f32[2,16,1,128]{3,2,1,0:T(1,128)S(1)}, f32[2,16,1,128]{3,2,1,0:T(1,128)S(1)}, u32[]{:S(2)}, u32[]{:S(2)}) collective-permute-start(f32[2,16,1,128]{3,2,1,0:T(1,128)S(1)} %get-tuple-element.126), channel_id=1, source_target_pairs={{1,0},{2,1},{3,2},{5,4},{6,5},{7,6},{9,8},{10,9},{11,10},{13,12},{... | collective-permute-start | bytes 49160 | tf_op jit(solution)/shard_map/ppermute | solution.py:26
  68.6 8.8 %collective-permute-start.18 = (f32[2,16,8,1]{3,2,1,0:T(8,128)S(1)}, f32[2,16,8,1]{3,2,1,0:T(8,128)S(1)}, u32[]{:S(2)}, u32[]{:S(2)}) collective-permute-start(f32[2,16,8,1]{3,2,1,0:T(8,128)S(1)} %get-tuple-element.117), channel_id=1, source_target_pairs={{0,4},{4,8},{8,12},{12,16},{16,20},{20,24},{24,28},{28,0},{1,5},{5... | collective-permute-start | bytes 3080 | tf_op jit(solution)/shard_map/ppermute | solution.py:23
  68.7 8.7 %collective-permute-start.19 = (f32[2,16,8,1]{3,2,1,0:T(8,128)S(1)}, f32[2,16,8,1]{3,2,1,0:T(8,128)S(1)}, u32[]{:S(2)}, u32[]{:S(2)}) collective-permute-start(f32[2,16,8,1]{3,2,1,0:T(8,128)S(1)} %get-tuple-element.118), channel_id=1, source_target_pairs={{4,0},{8,4},{12,8},{16,12},{20,16},{24,20},{28,24},{0,28},{5,1},{9... | collective-permute-start | bytes 3080 | tf_op jit(solution)/shard_map/ppermute | solution.py:26
  72.9 4.9 %collective-permute-start.20 = (f32[2,16,1,128]{3,2,1,0:T(1,128)S(1)}, f32[2,16,1,128]{3,2,1,0:T(1,128)S(1)}, u32[]{:S(2)}, u32[]{:S(2)}) collective-permute-start(f32[2,16,1,128]{3,2,1,0:T(1,128)S(1)} %get-tuple-element.113), channel_id=1, source_target_pairs={{0,1},{1,2},{2,3},{4,5},{5,6},{6,7},{8,9},{9,10},{10,11},{12,13},{... | collective-permute-start | bytes 49160 | tf_op jit(solution)/shard_map/ppermute | solution.py:23
  75.4 5.1 %collective-permute-start.21 = (f32[2,16,1,128]{3,2,1,0:T(1,128)S(1)}, f32[2,16,1,128]{3,2,1,0:T(1,128)S(1)}, u32[]{:S(2)}, u32[]{:S(2)}) collective-permute-start(f32[2,16,1,128]{3,2,1,0:T(1,128)S(1)} %get-tuple-element.114), channel_id=1, source_target_pairs={{1,0},{2,1},{3,2},{5,4},{6,5},{7,6},{9,8},{10,9},{11,10},{13,12},{... | collective-permute-start | bytes 49160 | tf_op jit(solution)/shard_map/ppermute | solution.py:26
  81.5 8.8 %collective-permute-start.22 = (f32[2,16,8,1]{3,2,1,0:T(8,128)S(1)}, f32[2,16,8,1]{3,2,1,0:T(8,128)S(1)}, u32[]{:S(2)}, u32[]{:S(2)}) collective-permute-start(f32[2,16,8,1]{3,2,1,0:T(8,128)S(1)} %get-tuple-element.109), channel_id=1, source_target_pairs={{0,4},{4,8},{8,12},{12,16},{16,20},{20,24},{24,28},{28,0},{1,5},{5... | collective-permute-start | bytes 3080 | tf_op jit(solution)/shard_map/ppermute | solution.py:23
  81.6 8.7 %collective-permute-start.23 = (f32[2,16,8,1]{3,2,1,0:T(8,128)S(1)}, f32[2,16,8,1]{3,2,1,0:T(8,128)S(1)}, u32[]{:S(2)}, u32[]{:S(2)}) collective-permute-start(f32[2,16,8,1]{3,2,1,0:T(8,128)S(1)} %get-tuple-element.110), channel_id=1, source_target_pairs={{4,0},{8,4},{12,8},{16,12},{20,16},{24,20},{28,24},{0,28},{5,1},{9... | collective-permute-start | bytes 3080 | tf_op jit(solution)/shard_map/ppermute | solution.py:26
  85.9 4.9 %collective-permute-start.24 = (f32[2,16,1,128]{3,2,1,0:T(1,128)S(1)}, f32[2,16,1,128]{3,2,1,0:T(1,128)S(1)}, u32[]{:S(2)}, u32[]{:S(2)}) collective-permute-start(f32[2,16,1,128]{3,2,1,0:T(1,128)S(1)} %get-tuple-element.105), channel_id=1, source_target_pairs={{0,1},{1,2},{2,3},{4,5},{5,6},{6,7},{8,9},{9,10},{10,11},{12,13},{... | collective-permute-start | bytes 49160 | tf_op jit(solution)/shard_map/ppermute | solution.py:23
  88.4 5.1 %collective-permute-start.25 = (f32[2,16,1,128]{3,2,1,0:T(1,128)S(1)}, f32[2,16,1,128]{3,2,1,0:T(1,128)S(1)}, u32[]{:S(2)}, u32[]{:S(2)}) collective-permute-start(f32[2,16,1,128]{3,2,1,0:T(1,128)S(1)} %get-tuple-element.106), channel_id=1, source_target_pairs={{1,0},{2,1},{3,2},{5,4},{6,5},{7,6},{9,8},{10,9},{11,10},{13,12},{... | collective-permute-start | bytes 49160 | tf_op jit(solution)/shard_map/ppermute | solution.py:26
  94.4 8.8 %collective-permute-start.26 = (f32[2,16,8,1]{3,2,1,0:T(8,128)S(1)}, f32[2,16,8,1]{3,2,1,0:T(8,128)S(1)}, u32[]{:S(2)}, u32[]{:S(2)}) collective-permute-start(f32[2,16,8,1]{3,2,1,0:T(8,128)S(1)} %get-tuple-element.101), channel_id=1, source_target_pairs={{0,4},{4,8},{8,12},{12,16},{16,20},{20,24},{24,28},{28,0},{1,5},{5... | collective-permute-start | bytes 3080 | tf_op jit(solution)/shard_map/ppermute | solution.py:23
  94.5 8.7 %collective-permute-start.27 = (f32[2,16,8,1]{3,2,1,0:T(8,128)S(1)}, f32[2,16,8,1]{3,2,1,0:T(8,128)S(1)}, u32[]{:S(2)}, u32[]{:S(2)}) collective-permute-start(f32[2,16,8,1]{3,2,1,0:T(8,128)S(1)} %get-tuple-element.102), channel_id=1, source_target_pairs={{4,0},{8,4},{12,8},{16,12},{20,16},{24,20},{28,24},{0,28},{5,1},{9... | collective-permute-start | bytes 3080 | tf_op jit(solution)/shard_map/ppermute | solution.py:26
  101.3 5.1 %collective-permute-start.29 = (f32[2,16,1,128]{3,2,1,0:T(1,128)S(1)}, f32[2,16,1,128]{3,2,1,0:T(1,128)S(1)}, u32[]{:S(2)}, u32[]{:S(2)}) collective-permute-start(f32[2,16,1,128]{3,2,1,0:T(1,128)S(1)} %get-tuple-element.98), channel_id=1, source_target_pairs={{1,0},{2,1},{3,2},{5,4},{6,5},{7,6},{9,8},{10,9},{11,10},{13,12},{... | collective-permute-start | bytes 49160 | tf_op jit(solution)/shard_map/ppermute | solution.py:26
  106.8 8.7 %collective-permute-start.30 = (f32[1,16,8,1]{3,2,1,0:T(8,128)S(1)}, f32[1,16,8,1]{3,2,1,0:T(8,128)S(1)}, u32[]{:S(2)}, u32[]{:S(2)}) collective-permute-start(f32[1,16,8,1]{3,2,1,0:T(8,128)S(1)} %get-tuple-element.155), channel_id=1, source_target_pairs={{0,4},{4,8},{8,12},{12,16},{16,20},{20,24},{24,28},{28,0},{1,5},{5... | collective-permute-start | bytes 1544 | tf_op jit(solution)/shard_map/ppermute | solution.py:23
  106.9 8.6 %collective-permute-start.31 = (f32[1,16,8,1]{3,2,1,0:T(8,128)S(1)}, f32[1,16,8,1]{3,2,1,0:T(8,128)S(1)}, u32[]{:S(2)}, u32[]{:S(2)}) collective-permute-start(f32[1,16,8,1]{3,2,1,0:T(8,128)S(1)} %get-tuple-element.156), channel_id=1, source_target_pairs={{4,0},{8,4},{12,8},{16,12},{20,16},{24,20},{28,24},{0,28},{5,1},{9... | collective-permute-start | bytes 1544 | tf_op jit(solution)/shard_map/ppermute | solution.py:26
  113.5 5.0 %collective-permute-start.33 = (f32[1,16,1,128]{3,2,1,0:T(1,128)S(1)}, f32[1,16,1,128]{3,2,1,0:T(1,128)S(1)}, u32[]{:S(2)}, u32[]{:S(2)}) collective-permute-start(f32[1,16,1,128]{3,2,1,0:T(1,128)S(1)} %get-tuple-element.158), channel_id=1, source_target_pairs={{1,0},{2,1},{3,2},{5,4},{6,5},{7,6},{9,8},{10,9},{11,10},{13,12},{... | collective-permute-start | bytes 24584 | tf_op jit(solution)/shard_map/ppermute | solution.py:26
  120.3 8.7 %collective-permute-start.34 = (f32[1,16,8,1]{3,2,1,0:T(8,128)S(1)}, f32[1,16,8,1]{3,2,1,0:T(8,128)S(1)}, u32[]{:S(2)}, u32[]{:S(2)}) collective-permute-start(f32[1,16,8,1]{3,2,1,0:T(8,128)S(1)} %get-tuple-element.151), channel_id=1, source_target_pairs={{0,4},{4,8},{8,12},{12,16},{16,20},{20,24},{24,28},{28,0},{1,5},{5... | collective-permute-start | bytes 1544 | tf_op jit(solution)/shard_map/ppermute | solution.py:23
  120.4 8.7 %collective-permute-start.35 = (f32[1,16,8,1]{3,2,1,0:T(8,128)S(1)}, f32[1,16,8,1]{3,2,1,0:T(8,128)S(1)}, u32[]{:S(2)}, u32[]{:S(2)}) collective-permute-start(f32[1,16,8,1]{3,2,1,0:T(8,128)S(1)} %get-tuple-element.152), channel_id=1, source_target_pairs={{4,0},{8,4},{12,8},{16,12},{20,16},{24,20},{28,24},{0,28},{5,1},{9... | collective-permute-start | bytes 1544 | tf_op jit(solution)/shard_map/ppermute | solution.py:26
  127.1 5.0 %collective-permute-start.37 = (f32[1,16,1,128]{3,2,1,0:T(1,128)S(1)}, f32[1,16,1,128]{3,2,1,0:T(1,128)S(1)}, u32[]{:S(2)}, u32[]{:S(2)}) collective-permute-start(f32[1,16,1,128]{3,2,1,0:T(1,128)S(1)} %get-tuple-element.154), channel_id=1, source_target_pairs={{1,0},{2,1},{3,2},{5,4},{6,5},{7,6},{9,8},{10,9},{11,10},{13,12},{... | collective-permute-start | bytes 24584 | tf_op jit(solution)/shard_map/ppermute | solution.py:26
  (18 other events, 54.7 us)
where the time goes:
time: 134 us; the launch traced here: 133 us
  starting transfers between devices  84.4 us (63%)
  waiting for transfers between devices  27 us (20%)
  other arithmetic  13.4 us (10%)
  local copies, waits for them, and re-layouts  5.56 us (4%)
  between operations  2.63 us (2%)
    ppermute x18, starting transfers between devices, extended(): lax.ppermute(lax.slice_in_dim(block, 0, width, axis=dim), axis, backward)  54.6 us
    ppermute x18, starting transfers between devices, extended(): lax.ppermute(lax.slice_in_dim(block, block.shape[dim] - width, None, axis...  24 us
    ppermute x18, waiting for transfers between devices, extended(): lax.ppermute(lax.slice_in_dim(block, 0, width, axis=dim), axis, backward)  23.9 us
    ppermute x1, starting transfers between devices, shifted_2(): return lax.ppermute(block, axis, route)  4.49 us
    unnamed x26, local copies, waits for them, and re-layouts  3.82 us
    ppermute x1, waiting for transfers between devices, shifted(): lax.ppermute(array, axis, [(i, (i + by) % size) for i in range(size)])  3.09 us
  transfers between devices with their start and end apart: 38, of which 10 were waited for; matrix products, arithmetic and copies ran while one was open for 4% of the time, Pallas kernels for 0%

commit v1 on v0

v1 whole, which is shorter than its diff:
```python
import functools
import math

import jax
import jax.numpy as jnp
from jax import lax
from jax.experimental import pallas as pl
from jax.experimental.pallas import tpu as pltpu
from jax.sharding import PartitionSpec as P

OUTER = 2
INNER = 4
DAY_STEPS = 96
RELAXATION = 0.7
FIELDS = 8

MESH = pl.DeviceIdType.MESH


def east_of(v, lane, lanes):
    r = pltpu.roll(v, lanes - 1, 2)
    return jnp.where(lane == lanes - 1, jnp.concatenate([r[1:], r[:1]], axis=0), r)


def west_of(v, lane, lanes):
    r = pltpu.roll(v, 1, 2)
    return jnp.where(lane == 0, jnp.concatenate([r[1:], r[:1]], axis=0), r)


def kernel(
    nx,
    ny,
    ckpt_h,
    traj_h,
    adjf_h,
    ed_h,
    nd_h,
    ew_h,
    nw_h,
    level_ref,
    damp_ref,
    source_h,
    obs_ref,
    weight_ref,
    step_ref,
    state_out,
    resid_out,
    adj_out,
    raw,
    pack_e,
    pack_w,
    recv_e,
    recv_w,
    pack1_e,
    pack1_w,
    recv1_e,
    recv1_w,
    pack2_e,
    pack2_w,
    recv2_e,
    recv2_w,
    coef,
    cf,
    x0,
    x1,
    x2,
    mu1,
    fw,
    fg,
    fd,
    fa,
    fb,
    aw,
    ag,
    ad,
    aa,
    ab,
    load_sem,
    send0,
    got0,
    sendl,
    gotl,
    send1,
    got1,
    send2,
    got2,
):
    levels, rows, lanes = state_out.shape
    wide = INNER
    ring = 2 * rows
    gx = lax.axis_index("gx")
    gy = lax.axis_index("gy")
    east = lax.rem(gx + 1, nx)
    west = lax.rem(gx + nx - 1, nx)
    has_n = gy < ny - 1
    has_s = gy > 0
    north = gy + 1
    south = gy - 1

    loads = [
        pltpu.make_async_copy(h, raw.at[f, :, pl.ds(0, rows), :], load_sem.at[f])
        for f, h in enumerate((ckpt_h, traj_h, adjf_h, ed_h, nd_h, ew_h, nw_h, source_h))
    ]
    for copy in loads:
        copy.start()

    barrier = pltpu.get_barrier_semaphore()

    zero_tile = jnp.zeros((rows, lanes), jnp.float32)

    def clear(l, carry):
        for f in range(FIELDS):
            raw[f, l, rows:, :] = zero_tile
        x1[l + 1, 0, rows:, :] = zero_tile
        mu1[l + 1, 0, rows:, :] = zero_tile
        x2[l + 1, 0, rows:, :] = zero_tile
        return carry

    lax.fori_loop(0, levels, clear, 0)
    for f in range(FIELDS):
        recv_e[f, rows:, :] = zero_tile
        recv_w[f, rows:, :] = zero_tile
    for f in range(2):
        recv1_e[f, rows:, :] = zero_tile
        recv1_w[f, rows:, :] = zero_tile
    recv2_e[rows:, :] = zero_tile
    recv2_w[rows:, :] = zero_tile
    zero_level = jnp.zeros((2, ring, lanes), jnp.float32)
    for ref in (x0, x1, x2, mu1, fa, fb, aa, ab):
        ref[0] = zero_level
        ref[levels + 1] = zero_level

    def greet(column, row):
        pl.semaphore_signal(barrier, inc=1, device_id={"gx": column, "gy": row}, device_id_type=MESH)

    greet(east, gy)
    greet(west, gy)

    @pl.when(has_n)
    def _():
        greet(gx, north)
        greet(east, north)
        greet(west, north)

    @pl.when(has_s)
    def _():
        greet(gx, south)
        greet(east, south)
        greet(west, south)

    pl.semaphore_wait(
        barrier, 2 + 3 * has_n.astype(jnp.int32) + 3 * has_s.astype(jnp.int32)
    )

    def remote(src, dst, send, got, column, row):
        return pltpu.make_async_remote_copy(
            src_ref=src,
            dst_ref=dst,
            send_sem=send,
            recv_sem=got,
            device_id={"gx": column, "gy": row},
            device_id_type=MESH,
        )

    low = pl.ds(0, wide)
    high = pl.ds(rows - wide, wide)
    from_n = pl.ds(rows, wide)
    from_s = pl.ds(ring - wide, wide)

    def lon_copies(pe, pw, re, rw, send, got):
        main = pl.ds(0, rows)
        return (
            [
                remote(pe, rw.at[..., main, :], send.at[0], got.at[0], east, gy),
                remote(pw, re.at[..., main, :], send.at[1], got.at[1], west, gy),
            ],
            [
                remote(
                    pe.at[..., high, :], rw.at[..., from_s, :], send.at[2], got.at[2], east, north
                ),
                remote(
                    pw.at[..., high, :], re.at[..., from_s, :], send.at[3], got.at[3], west, north
                ),
            ],
            [
                remote(
                    pe.at[..., low, :], rw.at[..., from_n, :], send.at[4], got.at[4], east, south
                ),
                remote(
                    pw.at[..., low, :], re.at[..., from_n, :], send.at[5], got.at[5], west, south
                ),
            ],
        )

    def lat_copies(refs, send, got):
        up = [
            remote(ref.at[..., high, :], ref.at[..., from_s, :], send.at[2 * k], got.at[2 * k], gx, north)
            for k, ref in enumerate(refs)
        ]
        down = [
            remote(ref.at[..., low, :], ref.at[..., from_n, :], send.at[2 * k + 1], got.at[2 * k + 1], gx, south)
            for k, ref in enumerate(refs)
        ]
        return up, down

    def start(up, down):
        if up:

            @pl.when(has_n)
            def _():
                for copy in up:
                    copy.start()

            @pl.when(has_s)
            def _():
                for copy in down:
                    copy.start()

    def arrive(up, down):
        @pl.when(has_s)
        def _():
            for copy in up:
                copy.wait_recv()

        @pl.when(has_n)
        def _():
            for copy in down:
                copy.wait_recv()

    def flush(up, down):
        @pl.when(has_n)
        def _():
            for copy in up:
                copy.wait_send()

        @pl.when(has_s)
        def _():
            for copy in down:
                copy.wait_send()

    lane2 = lax.broadcasted_iota(jnp.int32, (rows, lanes), 1)
    group = lane2 // wide
    laner = lax.broadcasted_iota(jnp.int32, (ring, lanes), 1)
    lane = lax.broadcasted_iota(jnp.int32, (2, ring, lanes), 2)
    side = lax.broadcasted_iota(jnp.int32, (2, ring, lanes), 0)
    row = lax.broadcasted_iota(jnp.int32, (2, ring, lanes), 1)

    def pack(tile, l, pe, pw):
        pe = jnp.where(group == l, pltpu.roll(tile, wide * l + wide, 1), pe)
        pw = jnp.where(group == l, pltpu.roll(tile, wide * l, 1), pw)
        return pe, pw

    def unpack(re, rw, l):
        e = pltpu.roll(re, lanes - wide * l, 1)
        w = pltpu.roll(rw, lanes - wide * l - wide, 1)
        return jnp.where(laner < wide, e, jnp.where(laner >= lanes - wide, w, 0.0))

    lat0 = [
        lat_copies([raw.at[f]], send0.at[pl.ds(2 * f, 2)], got0.at[pl.ds(2 * f, 2)])
        for f in range(FIELDS)
    ]
    for f in range(FIELDS):
        loads[f].wait()
        start(*lat0[f])

    def pack0(l, carry):
        out = []
        for f in range(FIELDS):
            out.extend(pack(raw[f, l, :rows, :], l, carry[2 * f], carry[2 * f + 1]))
        return tuple(out)

    packed = lax.fori_loop(0, levels, pack0, (zero_tile,) * (2 * FIELDS), unroll=True)
    for f in range(FIELDS):
        pack_e[f] = packed[2 * f]
        pack_w[f] = packed[2 * f + 1]
    lon0 = lon_copies(pack_e, pack_w, recv_e, recv_w, sendl.at[pl.ds(0, 6)], gotl.at[pl.ds(0, 6)])
    for copy in lon0[0]:
        copy.start()
    start(*lon0[1:])

    column = jnp.where(side == 0, lane, jnp.where(lane < lanes // 2, lane + lanes, lane - lanes))
    column = (gx * lanes + column).astype(jnp.float32)[:, :1]
    phase = (
        2.0 * math.pi * column / (lanes * nx)
        - 2.0 * math.pi * step_ref[0].astype(jnp.float32) / DAY_STEPS
    )
    heat = jnp.cos(phase)
    row_global = gy * rows + jnp.where(row < rows + wide, row, row - ring)
    open_face = (row_global >= 0) & (row_global < rows * ny - 1)

    def level_terms(l):
        up = jnp.where(l < levels - 1, level_ref[l], 0.0)
        down = jnp.where(l > 0, level_ref[jnp.maximum(l - 1, 0)], 0.0)
        return up, down, damp_ref[l]

    for up, down in lat0:
        arrive(up, down)
    for copy in lon0[0]:
        copy.wait_recv()
    arrive(*lon0[1:])

    def prepare(l, carry):
        def ext(f):
            halo = unpack(recv_e[f], recv_w[f], l)
            return jnp.stack([raw[f, l], halo])

        up, down, damp = level_terms(l)
        de = ext(3)
        fe = 0.5 * ext(5)
        dn = jnp.where(open_face, ext(4), 0.0)
        fn = jnp.where(open_face, 0.5 * ext(6), 0.0)
        a, b = fe + de, fe - de
        an, bn = fn + dn, fn - dn
        a_w = west_of(a, lane, lanes)
        b_w = west_of(b, lane, lanes)
        an_s = pltpu.roll(an, 1, 1)
        bn_s = pltpu.roll(bn, 1, 1)
        diag = 1.0 + (a - b_w) + (an - bn_s) + (up + down)
        total = 1.0 + de + 0.5 * (a_w - b_w) + dn + 0.5 * (an_s - bn_s) + (up + down)
        for k, value in enumerate((a, b, a_w, b_w, an, bn, an_s, bn_s, diag, total)):
            coef[k, l] = value
        x = ext(0)
        x0[l + 1] = x
        cf[l] = x + ext(7) * heat
        t = jnp.tanh(ext(1))
        local = damp * (1.0 - t * t)
        w = RELAXATION / (total + local)
        start_delta = w * ext(2)
        aw[l] = w
        ag[l] = 1.0 - w * (diag + local)
        ad[l] = start_delta
        aa[l + 1] = start_delta
        return carry

    lax.fori_loop(0, levels, prepare, 0, unroll=2)

    def off_forward(ref, l, up, down):
        v = ref[l + 1]
        off = (
            east_of(v, lane, lanes) * coef[1, l]
            - west_of(v, lane, lanes) * coef[2, l]
            + pltpu.roll(v, ring - 1, 1) * coef[5, l]
            - pltpu.roll(v, 1, 1) * coef[6, l]
            - up * ref[l + 2]
            - down * ref[l]
        )
        return v, off

    def off_adjoint(ref, l, up, down):
        v = ref[l + 1]
        off = (
            west_of(v, lane, lanes) * coef[3, l]
            - east_of(v, lane, lanes) * coef[0, l]
            + pltpu.roll(v, 1, 1) * coef[7, l]
            - pltpu.roll(v, ring - 1, 1) * coef[4, l]
            - up * ref[l + 2]
            - down * ref[l]
        )
        return v, off

    def resid_forward(x_ref, l):
        up, down, damp = level_terms(l)
        x, off = off_forward(x_ref, l, up, down)
        t = jnp.tanh(x)
        local = damp * (1.0 - t * t)
        diag = coef[8, l]
        r = x * diag + off + damp * t - cf[l]
        w = RELAXATION / (coef[9, l] + local)
        fw[l] = w
        fg[l] = 1.0 - w * (diag + local)
        fd[l] = -w * r
        fa[l + 1] = -w * r

    def resid_adjoint(m_ref, l):
        up, down, damp = level_terms(l)
        m, off = off_adjoint(m_ref, l, up, down)
        w = aw[l]
        d = carry_forcing[l] - (1.0 - ag[l]) * m - w * off
        ad2[l] = d
        aa[l + 1] = d

    def lin_forward(src, l):
        up, down, _ = level_terms(l)
        v, off = off_forward(src, l, up, down)
        return fg[l] * v + fd[l] - fw[l] * off

    def lin_adjoint(src, l, base):
        up, down, _ = level_terms(l)
        v, off = off_adjoint(src, l, up, down)
        return ag[l] * v + base[l] - aw[l] * off

    carry_forcing = ad
    ad2 = coef.at[9]

    def newton(x_ref, base):
        def sweep(f_src, f_dst, a_src, a_dst):
            def body(l, carry):
                f_dst[l + 1] = lin_forward(f_src, l)
                a_dst[l + 1] = lin_adjoint(a_src, l, base)
                return carry

            lax.fori_loop(0, levels, body, 0, unroll=2)

        pairs = [(fa, fb, aa, ab), (fb, fa, ab, aa)]
        for k in range(INNER - 2):
            sweep(*pairs[k % 2])
        return pairs[(INNER - 2) % 2]

    def first(l, carry):
        resid_forward(x0, l)
        return carry

    lax.fori_loop(0, levels, first, 0, unroll=2)
    last = newton(x0, ad)

    def close1(l, carry):
        xe, xw, me, mw = carry
        x = x0[l + 1, 0, :rows, :] + lin_forward(last[0], l)[0, :rows, :]
        m = lin_adjoint(last[2], l, ad)[0, :rows, :]
        x1[l + 1, 0, :rows, :] = x
        mu1[l + 1, 0, :rows, :] = m
        return pack(x, l, xe, xw) + pack(m, l, me, mw)

    xe, xw, me, mw = lax.fori_loop(0, levels, close1, (zero_tile,) * 4, unroll=2)
    pack1_e[0] = xe
    pack1_e[1] = me
    pack1_w[0] = xw
    pack1_w[1] = mw
    inside = pl.ds(1, levels)
    lon1 = lon_copies(
        pack1_e, pack1_w, recv1_e, recv1_w, sendl.at[pl.ds(6, 6)], gotl.at[pl.ds(6, 6)]
    )
    for copy in lon1[0]:
        copy.start()
    start(*lon1[1:])
    lat1 = lat_copies([x1.at[inside, 0], mu1.at[inside, 0]], send1, got1)
    start(*lat1)
    for copy in lon1[0]:
        copy.wait_recv()
    arrive(*lon1[1:])
    arrive(*lat1)

    def spread1(l, carry):
        x1[l + 1, 1] = unpack(recv1_e[0], recv1_w[0], l)
        mu1[l + 1, 1] = unpack(recv1_e[1], recv1_w[1], l)
        return carry

    lax.fori_loop(0, levels, spread1, 0, unroll=4)

    def second(l, carry):
        resid_forward(x1, l)
        resid_adjoint(mu1, l)
        return carry

    lax.fori_loop(0, levels, second, 0, unroll=2)
    last = newton(x1, ad2)

    def close2(l, carry):
        xe, xw = carry
        x = x1[l + 1, 0, :rows, :] + lin_forward(last[0], l)[0, :rows, :]
        m = mu1[l + 1, 0, :rows, :] + lin_adjoint(last[2], l, ad2)[0, :rows, :]
        x2[l + 1, 0, :rows, :] = x
        state_out[l] = x
        adj_out[l] = m + weight_ref[l] * (x - obs_ref[l])
        return pack(x, l, xe, xw)

    xe, xw = lax.fori_loop(0, levels, close2, (zero_tile,) * 2, unroll=2)
    pack2_e[...] = xe
    pack2_w[...] = xw
    main = pl.ds(0, rows)
    lon2 = [
        remote(pack2_e, recv2_w.at[main, :], sendl.at[12], gotl.at[12], east, gy),
        remote(pack2_w, recv2_e.at[main, :], sendl.at[13], gotl.at[13], west, gy),
    ]
    for copy in lon2:
        copy.start()
    lat2 = (
        [
            remote(
                x2.at[inside, 0, pl.ds(rows - 1, 1), :],
                x2.at[inside, 0, pl.ds(ring - 1, 1), :],
                send2.at[0], got2.at[0], gx, north,
            )
        ],
        [
            remote(
                x2.at[inside, 0, pl.ds(0, 1), :],
                x2.at[inside, 0, pl.ds(rows, 1), :],
                send2.at[1], got2.at[1], gx, south,
            )
        ],
    )
    start(*lat2)
    for copy in lon2:
        copy.wait_recv()
    arrive(*lat2)

    def finish(l, carry):
        x2[l + 1, 1] = unpack(recv2_e[...], recv2_w[...], l)
        up, down, damp = level_terms(l)
        x, off = off_forward(x2, l, up, down)
        r = x * coef[8, l] + off + damp * jnp.tanh(x) - cf[l]
        resid_out[l] = r[0, :rows, :]
        return carry

    lax.fori_loop(0, levels, finish, 0, unroll=2)

    for up, down in lat0:
        flush(up, down)
    flush(*lat1)
    flush(*lat2)
    for copy in lon0[0] + lon1[0] + lon2:
        copy.wait_send()
    flush(*lon0[1:])
    flush(*lon1[1:])


def solution(mesh):
    nx, ny = mesh.shape["gx"], mesh.shape["gy"]

    def per_device(*arrays):
        levels, rows, lanes = arrays[0].shape
        assert rows >= INNER and levels * INNER <= lanes
        ring = 2 * rows
        out = jax.ShapeDtypeStruct((levels, rows, lanes), jnp.float32)
        vmem = pl.BlockSpec(memory_space=pltpu.VMEM)
        smem = pl.BlockSpec(memory_space=pltpu.SMEM)
        hbm = pl.BlockSpec(memory_space=pl.ANY)
        f32 = jnp.float32

        def buf(*shape):
            return pltpu.VMEM(shape, f32)

        def padded():
            return buf(levels + 2, 2, ring, lanes)

        def full():
            return buf(levels, 2, ring, lanes)

        def dma(n):
            return pltpu.SemaphoreType.DMA((n,))

        return pl.pallas_call(
            functools.partial(kernel, nx, ny),
            name="step_pair",
            out_shape=(out, out, out),
            in_specs=[hbm] * 7 + [smem, smem, hbm, vmem, vmem, smem],
            out_specs=(vmem, vmem, vmem),
            scratch_shapes=[
                buf(FIELDS, levels, ring, lanes),
                buf(FIELDS, rows, lanes),
                buf(FIELDS, rows, lanes),
                buf(FIELDS, ring, lanes),
                buf(FIELDS, ring, lanes),
                buf(2, rows, lanes),
                buf(2, rows, lanes),
                buf(2, ring, lanes),
                buf(2, ring, lanes),
                buf(rows, lanes),
                buf(rows, lanes),
                buf(ring, lanes),
                buf(ring, lanes),
                buf(10, levels, 2, ring, lanes),
                full(),
                padded(),
                padded(),
                padded(),
                padded(),
                full(),
                full(),
                full(),
                padded(),
                padded(),
                full(),
                full(),
                full(),
                padded(),
                padded(),
                dma(FIELDS),
                dma(2 * FIELDS),
                dma(2 * FIELDS),
                dma(14),
                dma(14),
                dma(4),
                dma(4),
                dma(2),
                dma(2),
            ],
            compiler_params=pltpu.CompilerParams(
                collective_id=0, has_side_effects=True, vmem_limit_bytes=48 * 1024 * 1024
            ),
        )(*arrays)

    block = P(None, "gy", "gx")
    return jax.shard_map(
        per_device,
        mesh=mesh,
        in_specs=(block,) * 7 + (P(), P(), block, block, block, P()),
        out_specs=(block,) * 3,
        check_vma=False,
    )
```

time: 134 us -> 43.7 us (0.33)
  the two profiles are of different devices: /device:TPU:1 before, /device:TPU:0 now
where the time goes in v1:
time: 43.7 us; the launch traced here: 43.1 us
  Pallas kernels  31.5 us (72%)
  local copies, waits for them, and re-layouts  10.3 us (24%)
  between operations  1.36 us (3%)
    pallas_call x1, Pallas kernels, per_device(): pl.pallas_call(functools.partial(kernel, nx, ny), name='step_pair', out_s...  31.5 us
    unnamed x27, local copies, waits for them, and re-layouts  10.3 us

profile of v1, /device:TPU:0, one launch (start us, length us, event | category | flops | bytes accessed | tf_op | source)
XLA Modules:
  0.0 43.1 jit_solution(17360281035777445211)
XLA Ops:
  0.6 0.0 copy-start.11
  0.6 0.0 copy-start.10
  1.3 0.0 copy-done.11
  1.3 0.0 copy-done.10
  1.3 0.0 copy-start
  1.3 0.8 %copy-done = f32[16,8,128]{2,1,0:T(8,128)S(1)} copy-done((f32[16,8,128]{2,1,0:T(8,128)S(1)}, f32[16,8,128]{2,1,0:T(8,128)}, u32[]{:S(2)}) %copy-start) | copy-done | bytes 65560
  2.2 0.0 copy-start.1
  2.2 0.8 %copy-done.1 = f32[16,8,128]{2,1,0:T(8,128)S(1)} copy-done((f32[16,8,128]{2,1,0:T(8,128)S(1)}, f32[16,8,128]{2,1,0:T(8,128)}, u32[]{:S(2)}) %copy-start.1) | copy-done | bytes 65560
  3.0 0.0 copy-start.2
  3.0 0.8 %copy-done.2 = f32[16,8,128]{2,1,0:T(8,128)S(1)} copy-done((f32[16,8,128]{2,1,0:T(8,128)S(1)}, f32[16,8,128]{2,1,0:T(8,128)}, u32[]{:S(2)}) %copy-start.2) | copy-done | bytes 65560
  3.9 0.0 copy-start.3
  3.9 0.8 %copy-done.3 = f32[16,8,128]{2,1,0:T(8,128)S(1)} copy-done((f32[16,8,128]{2,1,0:T(8,128)S(1)}, f32[16,8,128]{2,1,0:T(8,128)}, u32[]{:S(2)}) %copy-start.3) | copy-done | bytes 65560
  4.7 0.0 copy-start.4
  4.7 0.8 %copy-done.4 = f32[16,8,128]{2,1,0:T(8,128)S(1)} copy-done((f32[16,8,128]{2,1,0:T(8,128)S(1)}, f32[16,8,128]{2,1,0:T(8,128)}, u32[]{:S(2)}) %copy-start.4) | copy-done | bytes 65560
  5.5 0.0 copy-start.5
  5.5 0.8 %copy-done.5 = f32[16,8,128]{2,1,0:T(8,128)S(1)} copy-done((f32[16,8,128]{2,1,0:T(8,128)S(1)}, f32[16,8,128]{2,1,0:T(8,128)}, u32[]{:S(2)}) %copy-start.5) | copy-done | bytes 65560
  6.4 0.0 copy-start.6
  6.4 0.8 %copy-done.6 = f32[16,8,128]{2,1,0:T(8,128)S(1)} copy-done((f32[16,8,128]{2,1,0:T(8,128)S(1)}, f32[16,8,128]{2,1,0:T(8,128)}, u32[]{:S(2)}) %copy-start.6) | copy-done | bytes 65560
  7.2 0.0 copy-start.7
  7.2 0.8 %copy-done.7 = f32[16,8,128]{2,1,0:T(8,128)S(1)} copy-done((f32[16,8,128]{2,1,0:T(8,128)S(1)}, f32[16,8,128]{2,1,0:T(8,128)}, u32[]{:S(2)}) %copy-start.7) | copy-done | bytes 65560
  8.1 0.0 copy-start.8
  8.1 0.8 %copy-done.8 = f32[16,8,128]{2,1,0:T(8,128)S(1)} copy-done((f32[16,8,128]{2,1,0:T(8,128)S(1)}, f32[16,8,128]{2,1,0:T(8,128)}, u32[]{:S(2)}) %copy-start.8) | copy-done | bytes 65560
  8.9 0.0 copy-start.9
  8.9 0.8 %copy-done.9 = f32[16,8,128]{2,1,0:T(8,128)S(1)} copy-done((f32[16,8,128]{2,1,0:T(8,128)S(1)}, f32[16,8,128]{2,1,0:T(8,128)}, u32[]{:S(2)}) %copy-start.9) | copy-done | bytes 65560
  9.7 31.5 %step_pair.1 = (f32[16,8,128]{2,1,0:T(8,128)S(1)}, f32[16,8,128]{2,1,0:T(8,128)S(1)}, f32[16,8,128]{2,1,0:T(8,128)S(1)}) custom-call(f32[16,8,128]{2,1,0:T(8,128)S(1)} %copy-done, f32[16,8,128]{2,1,0:T(8,128)S(1)} %copy-done.1, f32[16,8,128]{2,1,0:T(8,128)S(1)} %copy-done.2, f32[16,8,128]{2,1,0:T(8,128)S(1)} %copy-done.3, f32[16,8,128]{2,1,0:T(8,128)S(1)} %copy-done.4, ...), custom_call_target="tpu_custom_call" | custom-call | tf_op jit(solution)/shard_map/step_pair/pallas_call | solution.py:543
  41.2 0.6 %copy.20 = f32[16,8,128]{2,1,0:T(8,128)} copy(f32[16,8,128]{2,1,0:T(8,128)S(1)} %get-tuple-element.6) | data formatting | bytes 131072
  41.9 0.6 %copy.21 = f32[16,8,128]{2,1,0:T(8,128)} copy(f32[16,8,128]{2,1,0:T(8,128)S(1)} %get-tuple-element.7) | data formatting | bytes 131072
  42.5 0.6 %copy.22 = f32[16,8,128]{2,1,0:T(8,128)} copy(f32[16,8,128]{2,1,0:T(8,128)S(1)} %get-tuple-element.8) | data formatting | bytes 131072
Async XLA Ops:
  0.6 0.7 %copy-start.11 = (f32[16]{0:T(128)S(1)}, f32[16]{0:T(128)}, u32[]{:S(2)}) copy-start(f32[16]{0:T(128)} %damp_ref.1) | copy-start | bytes 196
  0.6 0.7 %copy-start.10 = (f32[16]{0:T(128)S(1)}, f32[16]{0:T(128)}, u32[]{:S(2)}) copy-start(f32[16]{0:T(128)} %level_ref.1) | copy-start | bytes 196
  1.3 0.8 %copy-start = (f32[16,8,128]{2,1,0:T(8,128)S(1)}, f32[16,8,128]{2,1,0:T(8,128)}, u32[]{:S(2)}) copy-start(f32[16,8,128]{2,1,0:T(8,128)} %ckpt_h.1) | copy-start | bytes 196612
  2.2 0.8 %copy-start.1 = (f32[16,8,128]{2,1,0:T(8,128)S(1)}, f32[16,8,128]{2,1,0:T(8,128)}, u32[]{:S(2)}) copy-start(f32[16,8,128]{2,1,0:T(8,128)} %traj_h.1) | copy-start | bytes 196612
  3.0 0.8 %copy-start.2 = (f32[16,8,128]{2,1,0:T(8,128)S(1)}, f32[16,8,128]{2,1,0:T(8,128)}, u32[]{:S(2)}) copy-start(f32[16,8,128]{2,1,0:T(8,128)} %adjf_h.1) | copy-start | bytes 196612
  3.9 0.8 %copy-start.3 = (f32[16,8,128]{2,1,0:T(8,128)S(1)}, f32[16,8,128]{2,1,0:T(8,128)}, u32[]{:S(2)}) copy-start(f32[16,8,128]{2,1,0:T(8,128)} %ed_h.1) | copy-start | bytes 196612
  4.7 0.8 %copy-start.4 = (f32[16,8,128]{2,1,0:T(8,128)S(1)}, f32[16,8,128]{2,1,0:T(8,128)}, u32[]{:S(2)}) copy-start(f32[16,8,128]{2,1,0:T(8,128)} %nd_h.1) | copy-start | bytes 196612
  5.5 0.8 %copy-start.5 = (f32[16,8,128]{2,1,0:T(8,128)S(1)}, f32[16,8,128]{2,1,0:T(8,128)}, u32[]{:S(2)}) copy-start(f32[16,8,128]{2,1,0:T(8,128)} %ew_h.1) | copy-start | bytes 196612
  6.4 0.8 %copy-start.6 = (f32[16,8,128]{2,1,0:T(8,128)S(1)}, f32[16,8,128]{2,1,0:T(8,128)}, u32[]{:S(2)}) copy-start(f32[16,8,128]{2,1,0:T(8,128)} %nw_h.1) | copy-start | bytes 196612
  7.2 0.8 %copy-start.7 = (f32[16,8,128]{2,1,0:T(8,128)S(1)}, f32[16,8,128]{2,1,0:T(8,128)}, u32[]{:S(2)}) copy-start(f32[16,8,128]{2,1,0:T(8,128)} %source_h.1) | copy-start | bytes 196612
  8.1 0.8 %copy-start.8 = (f32[16,8,128]{2,1,0:T(8,128)S(1)}, f32[16,8,128]{2,1,0:T(8,128)}, u32[]{:S(2)}) copy-start(f32[16,8,128]{2,1,0:T(8,128)} %obs_ref.1) | copy-start | bytes 196612
  8.9 0.8 %copy-start.9 = (f32[16,8,128]{2,1,0:T(8,128)S(1)}, f32[16,8,128]{2,1,0:T(8,128)}, u32[]{:S(2)}) copy-start(f32[16,8,128]{2,1,0:T(8,128)} %weight_ref.1) | copy-start | bytes 196612

commit v2 on v1

--- a/solution.py
+++ b/solution.py
@@ -37,12 +37,15 @@
     nd_h,
     ew_h,
     nw_h,
-    level_ref,
-    damp_ref,
+    level_h,
+    damp_h,
     source_h,
-    obs_ref,
-    weight_ref,
-    step_ref,
+    obs_h,
+    weight_h,
+    step_h,
+    state_h,
+    resid_h,
+    adj_h,
     state_out,
     resid_out,
     adj_out,
@@ -55,10 +58,6 @@
     pack1_w,
     recv1_e,
     recv1_w,
-    pack2_e,
-    pack2_w,
-    recv2_e,
-    recv2_w,
     coef,
     cf,
     x0,
@@ -75,6 +74,11 @@
     ad,
     aa,
     ab,
+    obs_ref,
+    weight_ref,
+    level_ref,
+    damp_ref,
+    step_ref,
     load_sem,
     send0,
     got0,
@@ -87,6 +91,7 @@
 ):
     levels, rows, lanes = state_out.shape
     wide = INNER
+    span = INNER + 1
     ring = 2 * rows
     gx = lax.axis_index("gx")
     gy = lax.axis_index("gy")
@@ -101,7 +106,16 @@
         pltpu.make_async_copy(h, raw.at[f, :, pl.ds(0, rows), :], load_sem.at[f])
         for f, h in enumerate((ckpt_h, traj_h, adjf_h, ed_h, nd_h, ew_h, nw_h, source_h))
     ]
-    for copy in loads:
+    late_loads = [
+        pltpu.make_async_copy(obs_h, obs_ref, load_sem.at[FIELDS]),
+        pltpu.make_async_copy(weight_h, weight_ref, load_sem.at[FIELDS + 1]),
+    ]
+    scalar_loads = [
+        pltpu.make_async_copy(level_h, level_ref, load_sem.at[FIELDS + 2]),
+        pltpu.make_async_copy(damp_h, damp_ref, load_sem.at[FIELDS + 3]),
+        pltpu.make_async_copy(step_h, step_ref, load_sem.at[FIELDS + 4]),
+    ]
+    for copy in loads + scalar_loads + late_loads:
         copy.start()
 
     barrier = pltpu.get_barrier_semaphore()
@@ -113,7 +127,7 @@
             raw[f, l, rows:, :] = zero_tile
         x1[l + 1, 0, rows:, :] = zero_tile
         mu1[l + 1, 0, rows:, :] = zero_tile
-        x2[l + 1, 0, rows:, :] = zero_tile
+        x2[l + 1, :, rows:, :] = jnp.zeros((2, rows, lanes), jnp.float32)
         return carry
 
     lax.fori_loop(0, levels, clear, 0)
@@ -123,8 +137,6 @@
     for f in range(2):
         recv1_e[f, rows:, :] = zero_tile
         recv1_w[f, rows:, :] = zero_tile
-    recv2_e[rows:, :] = zero_tile
-    recv2_w[rows:, :] = zero_tile
     zero_level = jnp.zeros((2, ring, lanes), jnp.float32)
     for ref in (x0, x1, x2, mu1, fa, fb, aa, ab):
         ref[0] = zero_level
@@ -239,21 +251,21 @@
                 copy.wait_send()
 
     lane2 = lax.broadcasted_iota(jnp.int32, (rows, lanes), 1)
-    group = lane2 // wide
+    group = lane2 // span
     laner = lax.broadcasted_iota(jnp.int32, (ring, lanes), 1)
     lane = lax.broadcasted_iota(jnp.int32, (2, ring, lanes), 2)
     side = lax.broadcasted_iota(jnp.int32, (2, ring, lanes), 0)
     row = lax.broadcasted_iota(jnp.int32, (2, ring, lanes), 1)
 
     def pack(tile, l, pe, pw):
-        pe = jnp.where(group == l, pltpu.roll(tile, wide * l + wide, 1), pe)
-        pw = jnp.where(group == l, pltpu.roll(tile, wide * l, 1), pw)
+        pe = jnp.where(group == l, pltpu.roll(tile, span * l + span, 1), pe)
+        pw = jnp.where(group == l, pltpu.roll(tile, span * l, 1), pw)
         return pe, pw
 
     def unpack(re, rw, l):
-        e = pltpu.roll(re, lanes - wide * l, 1)
-        w = pltpu.roll(rw, lanes - wide * l - wide, 1)
-        return jnp.where(laner < wide, e, jnp.where(laner >= lanes - wide, w, 0.0))
+        e = pltpu.roll(re, lanes - span * l, 1)
+        w = pltpu.roll(rw, lanes - span * l - span, 1)
+        return jnp.where(laner < span, e, jnp.where(laner >= lanes - span, w, 0.0))
 
     lat0 = [
         lat_copies([raw.at[f]], send0.at[pl.ds(2 * f, 2)], got0.at[pl.ds(2 * f, 2)])
@@ -278,6 +290,8 @@
         copy.start()
     start(*lon0[1:])
 
+    for copy in scalar_loads:
+        copy.wait()
     column = jnp.where(side == 0, lane, jnp.where(lane < lanes // 2, lane + lanes, lane - lanes))
     column = (gx * lanes + column).astype(jnp.float32)[:, :1]
     phase = (
@@ -332,7 +346,7 @@
         aa[l + 1] = start_delta
         return carry
 
-    lax.fori_loop(0, levels, prepare, 0, unroll=2)
+    lax.fori_loop(0, levels, prepare, 0, unroll=4)
 
     def off_forward(ref, l, up, down):
         v = ref[l + 1]
@@ -399,7 +413,7 @@
                 a_dst[l + 1] = lin_adjoint(a_src, l, base)
                 return carry
 
-            lax.fori_loop(0, levels, body, 0, unroll=2)
+            lax.fori_loop(0, levels, body, 0, unroll=4)
 
         pairs = [(fa, fb, aa, ab), (fb, fa, ab, aa)]
         for k in range(INNER - 2):
@@ -410,7 +424,7 @@
         resid_forward(x0, l)
         return carry
 
-    lax.fori_loop(0, levels, first, 0, unroll=2)
+    lax.fori_loop(0, levels, first, 0, unroll=4)
     last = newton(x0, ad)
 
     def close1(l, carry):
@@ -421,7 +435,7 @@
         mu1[l + 1, 0, :rows, :] = m
         return pack(x, l, xe, xw) + pack(m, l, me, mw)
 
-    xe, xw, me, mw = lax.fori_loop(0, levels, close1, (zero_tile,) * 4, unroll=2)
+    xe, xw, me, mw = lax.fori_loop(0, levels, close1, (zero_tile,) * 4, unroll=4)
     pack1_e[0] = xe
     pack1_e[1] = me
     pack1_w[0] = xw
@@ -452,28 +466,23 @@
         resid_adjoint(mu1, l)
         return carry
 
-    lax.fori_loop(0, levels, second, 0, unroll=2)
+    lax.fori_loop(0, levels, second, 0, unroll=4)
     last = newton(x1, ad2)
 
+    for copy in late_loads:
+        copy.wait()
+
     def close2(l, carry):
-        xe, xw = carry
-        x = x1[l + 1, 0, :rows, :] + lin_forward(last[0], l)[0, :rows, :]
+        xs = x1[l + 1, :, :rows, :] + lin_forward(last[0], l)[:, :rows, :]
         m = mu1[l + 1, 0, :rows, :] + lin_adjoint(last[2], l, ad2)[0, :rows, :]
-        x2[l + 1, 0, :rows, :] = x
+        x2[l + 1, 0, :rows, :] = xs[0]
+        x2[l + 1, 1, :rows, :] = xs[1]
+        x = xs[0]
         state_out[l] = x
         adj_out[l] = m + weight_ref[l] * (x - obs_ref[l])
-        return pack(x, l, xe, xw)
-
-    xe, xw = lax.fori_loop(0, levels, close2, (zero_tile,) * 2, unroll=2)
-    pack2_e[...] = xe
-    pack2_w[...] = xw
-    main = pl.ds(0, rows)
-    lon2 = [
-        remote(pack2_e, recv2_w.at[main, :], sendl.at[12], gotl.at[12], east, gy),
-        remote(pack2_w, recv2_e.at[main, :], sendl.at[13], gotl.at[13], west, gy),
-    ]
-    for copy in lon2:
-        copy.start()
+        return carry
+
+    lax.fori_loop(0, levels, close2, 0, unroll=4)
     lat2 = (
         [
             remote(
@@ -491,28 +500,49 @@
         ],
     )
     start(*lat2)
-    for copy in lon2:
-        copy.wait_recv()
+    stores = [
+        pltpu.make_async_copy(state_out, state_h, load_sem.at[0]),
+        pltpu.make_async_copy(adj_out, adj_h, load_sem.at[1]),
+        pltpu.make_async_copy(resid_out, resid_h, load_sem.at[2]),
+    ]
+    stores[0].start()
+    stores[1].start()
     arrive(*lat2)
 
     def finish(l, carry):
-        x2[l + 1, 1] = unpack(recv2_e[...], recv2_w[...], l)
         up, down, damp = level_terms(l)
         x, off = off_forward(x2, l, up, down)
         r = x * coef[8, l] + off + damp * jnp.tanh(x) - cf[l]
         resid_out[l] = r[0, :rows, :]
         return carry
 
-    lax.fori_loop(0, levels, finish, 0, unroll=2)
+    lax.fori_loop(0, levels, finish, 0, unroll=4)
+    stores[2].start()
 
     for up, down in lat0:
         flush(up, down)
     flush(*lat1)
     flush(*lat2)
-    for copy in lon0[0] + lon1[0] + lon2:
+    for copy in lon0[0] + lon1[0]:
         copy.wait_send()
     flush(*lon0[1:])
     flush(*lon1[1:])
+    for copy in stores:
+        copy.wait()
+
+
+def hand_over(a, b, c, x, y, z, held, sem):
+    takes = [pltpu.make_async_copy(ref, held.at[k], sem.at[k]) for k, ref in enumerate((a, b, c))]
+    gives = [
+        pltpu.make_async_copy(held.at[k], ref, sem.at[k + 3]) for k, ref in enumerate((x, y, z))
+    ]
+    for copy in takes:
+        copy.start()
+    for take, give in zip(takes, gives):
+        take.wait()
+        give.start()
+    for copy in gives:
+        copy.wait()
 
 
 def solution(mesh):
@@ -520,12 +550,10 @@
 
     def per_device(*arrays):
         levels, rows, lanes = arrays[0].shape
-        assert rows >= INNER and levels * INNER <= lanes
+        assert rows >= INNER and levels * (INNER + 1) <= lanes
         ring = 2 * rows
         out = jax.ShapeDtypeStruct((levels, rows, lanes), jnp.float32)
-        vmem = pl.BlockSpec(memory_space=pltpu.VMEM)
-        smem = pl.BlockSpec(memory_space=pltpu.SMEM)
-        hbm = pl.BlockSpec(memory_space=pl.ANY)
+        hbm = pl.BlockSpec(memory_space=pltpu.HBM)
         f32 = jnp.float32
 
         def buf(*shape):
@@ -540,13 +568,16 @@
         def dma(n):
             return pltpu.SemaphoreType.DMA((n,))
 
-        return pl.pallas_call(
+        results = pl.pallas_call(
             functools.partial(kernel, nx, ny),
             name="step_pair",
             out_shape=(out, out, out),
-            in_specs=[hbm] * 7 + [smem, smem, hbm, vmem, vmem, smem],
-            out_specs=(vmem, vmem, vmem),
+            in_specs=[hbm] * 13,
+            out_specs=(hbm, hbm, hbm),
             scratch_shapes=[
+                buf(levels, rows, lanes),
+                buf(levels, rows, lanes),
+                buf(levels, rows, lanes),
                 buf(FIELDS, levels, ring, lanes),
                 buf(FIELDS, rows, lanes),
                 buf(FIELDS, rows, lanes),
@@ -556,10 +587,6 @@
                 buf(2, rows, lanes),
                 buf(2, ring, lanes),
                 buf(2, ring, lanes),
-                buf(rows, lanes),
-                buf(rows, lanes),
-                buf(ring, lanes),
-                buf(ring, lanes),
                 buf(10, levels, 2, ring, lanes),
                 full(),
                 padded(),
@@ -576,20 +603,34 @@
                 full(),
                 padded(),
                 padded(),
-                dma(FIELDS),
+                buf(levels, rows, lanes),
+                buf(levels, rows, lanes),
+                pltpu.SMEM((levels,), f32),
+                pltpu.SMEM((levels,), f32),
+                pltpu.SMEM((1,), jnp.int32),
+                dma(FIELDS + 5),
                 dma(2 * FIELDS),
                 dma(2 * FIELDS),
-                dma(14),
-                dma(14),
+                dma(12),
+                dma(12),
                 dma(4),
                 dma(4),
                 dma(2),
                 dma(2),
             ],
             compiler_params=pltpu.CompilerParams(
-                collective_id=0, has_side_effects=True, vmem_limit_bytes=48 * 1024 * 1024
+                collective_id=0, has_side_effects=True, vmem_limit_bytes=67043328
             ),
         )(*arrays)
+        return pl.pallas_call(
+            hand_over,
+            name="hand_over",
+            out_shape=(out, out, out),
+            in_specs=[hbm] * 3,
+            out_specs=(hbm, hbm, hbm),
+            scratch_shapes=[buf(3, levels, rows, lanes), dma(6)],
+            compiler_params=pltpu.CompilerParams(vmem_limit_bytes=67043328),
+        )(*results)
 
     block = P(None, "gy", "gx")
     return jax.shard_map(

time: 43.7 us -> 29.1 us (0.67)
  the two profiles are of different devices: /device:TPU:0 before, /device:TPU:1 now
where the time goes in v2:
time: 29.1 us; the launch traced here: 28.9 us
  Pallas kernels  27.6 us (95%)
  between operations  1.29 us (4%)
    pallas_call x1, Pallas kernels, per_device(): pl.pallas_call(functools.partial(kernel, nx, ny), name='step_pair', out_s...  26 us
    pallas_call x1, Pallas kernels, per_device(): pl.pallas_call(hand_over, name='hand_over', out_shape=(out, out, out), in...  1.58 us

profile of v2, /device:TPU:1, one launch (start us, length us, event | category | flops | bytes accessed | tf_op | source)
XLA Modules:
  0.0 28.9 jit_solution(7273749634187584313)
XLA Ops:
  1.3 26.0 %step_pair.1 = (f32[16,8,128]{2,1,0:T(8,128)}, f32[16,8,128]{2,1,0:T(8,128)}, f32[16,8,128]{2,1,0:T(8,128)}) custom-call(f32[16,8,128]{2,1,0:T(8,128)} %ckpt_h.1, f32[16,8,128]{2,1,0:T(8,128)} %traj_h.1, f32[16,8,128]{2,1,0:T(8,128)} %adjf_h.1, f32[16,8,128]{2,1,0:T(8,128)} %ed_h.1, f32[16,8,128]{2,1,0:T(8,128)} %nd_h.1, f32[16,8,128]{2,1,0:T(8,128)} %ew_h.1, ...), custom_call_target="tpu_custom_call" | custom-call | tf_op jit(solution)/shard_map/step_pair/pallas_call | solution.py:571
  27.3 1.6 %hand_over.1 = (f32[16,8,128]{2,1,0:T(8,128)}, f32[16,8,128]{2,1,0:T(8,128)}, f32[16,8,128]{2,1,0:T(8,128)}) custom-call(f32[16,8,128]{2,1,0:T(8,128)} %get-tuple-element.6.a, f32[16,8,128]{2,1,0:T(8,128)} %get-tuple-element.7.b, f32[16,8,128]{2,1,0:T(8,128)} %get-tuple-element.8.c), custom_call_target="tpu_custom_call" | custom-call | tf_op jit(solution)/shard_map/hand_over/pallas_call | solution.py:625

commit v3 on v2

--- a/solution.py
+++ b/solution.py
@@ -346,7 +346,7 @@
         aa[l + 1] = start_delta
         return carry
 
-    lax.fori_loop(0, levels, prepare, 0, unroll=4)
+    lax.fori_loop(0, levels, prepare, 0, unroll=8)
 
     def off_forward(ref, l, up, down):
         v = ref[l + 1]
@@ -413,7 +413,7 @@
                 a_dst[l + 1] = lin_adjoint(a_src, l, base)
                 return carry
 
-            lax.fori_loop(0, levels, body, 0, unroll=4)
+            lax.fori_loop(0, levels, body, 0, unroll=8)
 
         pairs = [(fa, fb, aa, ab), (fb, fa, ab, aa)]
         for k in range(INNER - 2):
@@ -424,7 +424,7 @@
         resid_forward(x0, l)
         return carry
 
-    lax.fori_loop(0, levels, first, 0, unroll=4)
+    lax.fori_loop(0, levels, first, 0, unroll=8)
     last = newton(x0, ad)
 
     def close1(l, carry):
@@ -435,7 +435,7 @@
         mu1[l + 1, 0, :rows, :] = m
         return pack(x, l, xe, xw) + pack(m, l, me, mw)
 
-    xe, xw, me, mw = lax.fori_loop(0, levels, close1, (zero_tile,) * 4, unroll=4)
+    xe, xw, me, mw = lax.fori_loop(0, levels, close1, (zero_tile,) * 4, unroll=8)
     pack1_e[0] = xe
     pack1_e[1] = me
     pack1_w[0] = xw
@@ -459,14 +459,14 @@
         mu1[l + 1, 1] = unpack(recv1_e[1], recv1_w[1], l)
         return carry
 
-    lax.fori_loop(0, levels, spread1, 0, unroll=4)
+    lax.fori_loop(0, levels, spread1, 0, unroll=8)
 
     def second(l, carry):
         resid_forward(x1, l)
         resid_adjoint(mu1, l)
         return carry
 
-    lax.fori_loop(0, levels, second, 0, unroll=4)
+    lax.fori_loop(0, levels, second, 0, unroll=8)
     last = newton(x1, ad2)
 
     for copy in late_loads:
@@ -482,7 +482,7 @@
         adj_out[l] = m + weight_ref[l] * (x - obs_ref[l])
         return carry
 
-    lax.fori_loop(0, levels, close2, 0, unroll=4)
+    lax.fori_loop(0, levels, close2, 0, unroll=8)
     lat2 = (
         [
             remote(
@@ -516,7 +516,7 @@
         resid_out[l] = r[0, :rows, :]
         return carry
 
-    lax.fori_loop(0, levels, finish, 0, unroll=4)
+    lax.fori_loop(0, levels, finish, 0, unroll=8)
     stores[2].start()
 
     for up, down in lat0:

time: 29.1 us -> 27.8 us (0.955)
  Pallas kernels: 27.6 us -> 26.3 us
    pallas_call x1, Pallas kernels: 26 us -> 24.8 us  [per_device(): pl.pallas_call(functools.partial(kernel, nx, ny), name='step_pair', out_s...]
where the time goes in v3:
time: 27.8 us; the launch traced here: 27.6 us
  Pallas kernels  26.3 us (95%)
  between operations  1.29 us (5%)
    pallas_call x1, Pallas kernels, per_device(): pl.pallas_call(functools.partial(kernel, nx, ny), name='step_pair', out_s...  24.8 us
    pallas_call x1, Pallas kernels, per_device(): pl.pallas_call(hand_over, name='hand_over', out_shape=(out, out, out), in...  1.58 us

profile of v3, /device:TPU:1, one launch (start us, length us, event | category | flops | bytes accessed | tf_op | source)
XLA Modules:
  0.0 27.6 jit_solution(3646511094408794450)
XLA Ops:
  1.3 24.8 %step_pair.1 = (f32[16,8,128]{2,1,0:T(8,128)}, f32[16,8,128]{2,1,0:T(8,128)}, f32[16,8,128]{2,1,0:T(8,128)}) custom-call(f32[16,8,128]{2,1,0:T(8,128)} %ckpt_h.1, f32[16,8,128]{2,1,0:T(8,128)} %traj_h.1, f32[16,8,128]{2,1,0:T(8,128)} %adjf_h.1, f32[16,8,128]{2,1,0:T(8,128)} %ed_h.1, f32[16,8,128]{2,1,0:T(8,128)} %nd_h.1, f32[16,8,128]{2,1,0:T(8,128)} %ew_h.1, ...), custom_call_target="tpu_custom_call" | custom-call | tf_op jit(solution)/shard_map/step_pair/pallas_call | solution.py:571
  26.0 1.6 %hand_over.1 = (f32[16,8,128]{2,1,0:T(8,128)}, f32[16,8,128]{2,1,0:T(8,128)}, f32[16,8,128]{2,1,0:T(8,128)}) custom-call(f32[16,8,128]{2,1,0:T(8,128)} %get-tuple-element.6.a, f32[16,8,128]{2,1,0:T(8,128)} %get-tuple-element.7.b, f32[16,8,128]{2,1,0:T(8,128)} %get-tuple-element.8.c), custom_call_target="tpu_custom_call" | custom-call | tf_op jit(solution)/shard_map/hand_over/pallas_call | solution.py:625
